TPU v7x, 32 devices: a whole 2x2x4 slice. The times are simulated.
32 devices in a mesh: fsdp: 8 (over z, y), ctx: 4 (over x, core).
Axes of the slice: x: 2, y: 2, z: 4, core: 2. Of those that a mesh axis runs over, the one named last changes fastest.
Arguments:
- tokens: bfloat16 [32768, 1024], P(('fsdp', 'ctx')), may hold values from -6 to 6
- valid_mask: int32 [32768], P(('fsdp', 'ctx')), may hold values from 0 to 1, as said below
- stretch_start: int32 [128], P(('fsdp', 'ctx')), may hold values from 0 to 1, as said below
- cotangent: bfloat16 [32768, 1024], P(('fsdp', 'ctx')), may hold values from -6 to 6
- norm_gain: float32 [1024], replicated, may hold values from 0.1 to 1.9
- in_weight: bfloat16 [1024, 4384], P(('fsdp', 'ctx')), may hold values from -0.1875 to 0.1875
- conv_weight: float32 [4, 2304], replicated, may hold values from -2 to 2
- conv_bias: float32 [2304], replicated, may hold values from -0.5 to 0.5
- step_bias: float32 [32], replicated, may hold values from -6 to -2
- decay_log: float32 [32], replicated, may hold values from -5 to 1.5
- skip_gain: float32 [32], replicated, may hold values from 0.5 to 1.5
- gate_gain: float32 [2048], replicated, may hold values from 0.1 to 1.9
- out_weight: bfloat16 [2048, 1024], P(('fsdp', 'ctx')), may hold values from -0.125 to 0.125
Outputs:
- output: bfloat16 [32768, 1024], P(('fsdp', 'ctx'))
- input_grad: float32 [32768, 1024], P(('fsdp', 'ctx'))
- in_weight_grad: float32 [1024, 4384], P(('fsdp', 'ctx'))
- out_weight_grad: float32 [2048, 1024], P(('fsdp', 'ctx'))
- norm_gain_grad: float32 [1024], replicated
- conv_weight_grad: float32 [4, 2304], replicated
- conv_bias_grad: float32 [2304], replicated
- step_bias_grad: float32 [32], replicated
- decay_log_grad: float32 [32], replicated
- skip_gain_grad: float32 [32], replicated
- gate_gain_grad: float32 [2048], replicated
Inputs may be any that keep to these rules, and one draw needn't show every extreme that they name: `stretch_start`: each group of 4096 tokens holds whole sequences laid end to end, each beginning at a stretch of 256 tokens; a sequence's first stretch lies a multiple of 4 stretches into its group, so the group's first stretch always begins one. A sequence's padding is only the tail of its last stretch; each sequence has 1024 tokens or more. `valid_mask`: 1 exactly for the tokens of sequences as described for stretch_start.
All inputs are finite; a program needn't handle non-finite values.
Results may differ from a plain program's by a relative error of at most 0.0092.
Values may be sent and summed in bfloat16 or wider, within the bound.
A program may use at most 320 MiB of HBM per device.

v0:
```python
import jax
import jax.numpy as jnp
from jax import lax
from jax.sharding import PartitionSpec as P

DI = 2048
HEADS = 32
P_SIZE = 64
N = 128
CONVK = 4
Q = 256
CH = 2304
DPROJ = 4384


epsilon = 1e-05


def passed_along(shard, axis, by):
    length = lax.axis_size(axis)
    pairs = [(i, i + by) for i in range(length) if 0 <= i + by < length]
    return lax.ppermute(shard, axis, pairs)


def entering_2(shard, axis, join, neutral):
    place = lax.axis_index(axis)
    gathered = jax.tree.map(
        lambda a, kind: lax.all_gather(a.astype(kind), axis),
        shard,
        jax.tree.map(lambda a: jnp.bfloat16 if a.dtype == jnp.float32 else a.dtype, shard),
    )
    state = jax.tree.map(lambda a, e: jnp.zeros_like(a) + jnp.asarray(e, a.dtype), shard, neutral)

    def one(step, state):
        return join(
            state,
            jax.tree.map(
                lambda a, own: lax.dynamic_index_in_dim(a, step, 0, False).astype(own.dtype),
                gathered,
                shard,
            ),
        )

    return lax.fori_loop(0, place, one, state)


def entering_3(shard, axis, combine, identity):
    length, position = (lax.axis_size(axis), lax.axis_index(axis))
    everything = jax.tree.map(lambda part: lax.all_gather(part, axis), shard)
    start = jax.tree.map(
        lambda part, zero: jnp.broadcast_to(jnp.asarray(zero, part.dtype), part.shape),
        shard,
        identity,
    )

    def step(k, before):
        at = length - 1 - k
        reached = at > position
        new = combine(before, jax.tree.map(lambda part: part[at], everything))
        return jax.tree.map(lambda a, b: jnp.where(reached, a, b), new, before)

    return lax.fori_loop(0, length, step, start)


def make_rounders():

    def value_plain(v):
        return lax.optimization_barrier(v.astype(jnp.bfloat16)).astype(jnp.float32)

    round_value = jax.custom_vjp(value_plain)

    def value_keep(v):
        return (round_value(v), None)

    def value_pass(kept, grad):
        return (grad,)

    round_value.defvjp(value_keep, value_pass)

    def grad_plain(v):
        return v

    round_grad = jax.custom_vjp(grad_plain)

    def grad_keep(v):
        return (v, None)

    def grad_round(kept, grad):
        return (round_value(grad),)

    round_grad.defvjp(grad_keep, grad_round)
    return (round_value, round_grad)


def rms_scale(values_in, gain):
    return (
        values_in
        * lax.rsqrt(jnp.mean(values_in * values_in, axis=-1, keepdims=True) + epsilon)
        * gain
    )


def lower_ones(length):
    return (jnp.arange(length)[:, None] >= jnp.arange(length)[None, :]).astype(jnp.float32)


def first_section(
    blocked,
    edge_rows,
    keep_state,
    valid_blocks,
    conv_weight,
    conv_bias,
    step_bias,
    decay_log,
    rounders,
):
    round_value, round_grad = rounders
    stretches = blocked.shape[0]
    width = blocked.shape[1]
    gate_in = blocked[:, :, :DI]
    conv_in = blocked[:, :, DI : DI + CH]
    step_raw = blocked[:, :, DI + CH :]
    tail_rows = CONVK - 1
    history = (
        jnp.concatenate([edge_rows[None], conv_in[:-1, width - tail_rows :]], axis=0)
        * keep_state[:, None, None]
    )
    padded = jnp.concatenate([history, conv_in], axis=1)
    convolved = conv_bias + jnp.zeros_like(conv_in)
    for offset in range(CONVK):
        convolved = convolved + conv_weight[offset] * padded[:, offset : offset + width]
    activated = jax.nn.silu(convolved)
    values = activated[:, :, :DI].reshape(stretches, width, HEADS, P_SIZE)
    in_map = activated[:, :, DI : DI + N]
    out_map = activated[:, :, DI + N :]
    step_size = jax.nn.softplus(step_raw + step_bias) * valid_blocks[:, :, None]
    decay_rate = -jnp.exp(decay_log)
    log_decay = jnp.einsum(
        "qs,csh->chq", lower_ones(width), step_size * decay_rate, precision=lax.Precision.HIGHEST
    )
    values_low = round_value(values)
    in_low = round_value(in_map)
    out_low = round_value(out_map)
    intersection = round_grad(jnp.einsum("cqn,csn->cqs", out_low, in_low))
    causal = lower_ones(width) > 0.5
    log_ratio = log_decay[:, :, :, None] - log_decay[:, :, None, :]
    decay_map = jnp.where(causal, jnp.exp(jnp.where(causal, log_ratio, 0.0)), 0.0)
    step_heads = jnp.swapaxes(step_size, 1, 2)
    mixing = round_value(intersection[:, None] * decay_map * step_heads[:, :, None, :])
    local_out = jnp.einsum("chqs,cshp->cqhp", mixing, values_low)
    log_total = log_decay[:, :, -1]
    state_weight = jnp.exp(log_total[:, :, None] - log_decay) * step_heads
    weighted = round_value(values * jnp.swapaxes(state_weight, 1, 2)[:, :, :, None])
    stretch_states = round_grad(jnp.einsum("cshp,csn->chpn", weighted, in_low))
    stretch_decay = jnp.exp(log_total)
    return (local_out, values, out_low, log_decay, stretch_states, stretch_decay, gate_in)


def second_section(
    local_out,
    values,
    out_low,
    log_decay,
    stretch_states,
    stretch_decay,
    gate_in,
    keep_state,
    start_state,
    skip_gain,
    gate_gain,
    rounders,
):
    round_value, round_grad = rounders

    def advance(carried, element):
        state_in, decay_in, keep_in = element
        entering_now = keep_in * carried
        return (decay_in[:, None, None] * entering_now + state_in, entering_now)

    unused, entering = lax.scan(advance, start_state, (stretch_states, stretch_decay, keep_state))
    part = round_grad(jnp.einsum("cqn,chpn->cqhp", out_low, round_value(entering)))
    remote_out = part * jnp.swapaxes(jnp.exp(log_decay), 1, 2)[:, :, :, None]
    ssd_out = round_grad(local_out + remote_out + skip_gain[:, None] * values)
    row_count = ssd_out.shape[0] * ssd_out.shape[1]
    mixed = ssd_out.reshape(row_count, DI) * jax.nn.silu(gate_in.reshape(row_count, DI))
    return round_value(rms_scale(mixed, gate_gain))


def link(earlier, later):
    return (earlier[0] * later[0], later[1] + later[0][:, None, None] * earlier[1])


def local(
    tokens,
    valid_mask,
    stretch_start,
    cotangent,
    norm_gain,
    in_weight,
    conv_weight,
    conv_bias,
    step_bias,
    decay_log,
    skip_gain,
    gate_gain,
    out_weight,
):
    rounders = make_rounders()
    in_full, out_full = (
        lax.all_gather(in_weight, ("fsdp", "ctx"), axis=0, tiled=True),
        lax.all_gather(out_weight, ("fsdp", "ctx"), axis=0, tiled=True),
    )
    rows_here = tokens.shape[0]
    blocks = rows_here // Q
    inputs32 = tokens.astype(jnp.float32)
    validity = valid_mask.astype(jnp.float32)
    valid_blocks = validity.reshape(blocks, Q)
    keep_state = 1.0 - stretch_start.astype(jnp.float32)
    normed, norm_back = jax.vjp(rms_scale, inputs32, norm_gain)
    normed_low = normed.astype(jnp.bfloat16)
    projected = jnp.dot(normed_low, in_full, preferred_element_type=jnp.float32)
    edge_rows = passed_along(projected[rows_here - (CONVK - 1) :, DI : DI + CH], "ctx", 1)

    def first_part(blocked, edge_in, conv_taps, conv_shift, step_shift, decay_logs):
        pieces = first_section(
            blocked,
            edge_in,
            keep_state,
            valid_blocks,
            conv_taps,
            conv_shift,
            step_shift,
            decay_logs,
            rounders,
        )
        states_here = pieces[4]
        decays_here = pieces[5]
        device_decay = jnp.ones((HEADS,), jnp.float32)
        device_state = jnp.zeros((HEADS, P_SIZE, N), jnp.float32)
        for position in range(blocks):
            factor = decays_here[position] * keep_state[position]
            device_state = states_here[position] + factor[:, None, None] * device_state
            device_decay = device_decay * factor
        return pieces + (device_decay, device_state)

    firsts, first_back = jax.vjp(
        first_part,
        projected.reshape(blocks, Q, DPROJ),
        edge_rows,
        conv_weight,
        conv_bias,
        step_bias,
        decay_log,
    )
    device_decay = firsts[7]
    device_state = firsts[8]
    identity = (jnp.ones((HEADS,), jnp.float32), jnp.zeros((HEADS, P_SIZE, N), jnp.float32))
    start_state = entering_2((device_decay, device_state), "ctx", link, identity)[1]

    def second_part(
        local_out,
        values,
        out_low,
        log_decay,
        stretch_states,
        stretch_decay,
        gate_in,
        state_in,
        skip_in,
        gain_in,
    ):
        return second_section(
            local_out,
            values,
            out_low,
            log_decay,
            stretch_states,
            stretch_decay,
            gate_in,
            keep_state,
            state_in,
            skip_in,
            gain_in,
            rounders,
        )

    gated, second_back = jax.vjp(second_part, *firsts[:7], start_state, skip_gain, gate_gain)
    gated_low = gated.astype(jnp.bfloat16)
    branch = jnp.dot(gated_low, out_full, preferred_element_type=jnp.float32)
    output = (inputs32 + validity[:, None] * branch).astype(jnp.bfloat16)
    cot32 = cotangent.astype(jnp.float32)
    branch_grad = (cot32 * validity[:, None]).astype(jnp.bfloat16)
    back_in, back_out = (
        lax.all_gather(in_weight, ("fsdp", "ctx"), axis=0, tiled=True),
        lax.all_gather(out_weight, ("fsdp", "ctx"), axis=0, tiled=True),
    )
    shard_count = lax.axis_size(("fsdp", "ctx"))
    gated_grad = lax.dot_general(
        branch_grad, back_out, (((1,), (1,)), ((), ())), preferred_element_type=jnp.float32
    )
    columns = lax.slice_in_dim(
        gated_low, 0, DI // shard_count * lax.axis_size(("fsdp", "ctx")), axis=1
    )
    out_weight_grad = lax.psum_scatter(
        lax.dot_general(
            columns, branch_grad, (((0,), (0,)), ((), ())), preferred_element_type=jnp.float32
        ),
        ("fsdp", "ctx"),
        scatter_dimension=0,
        tiled=True,
    )
    seconds = second_back(gated_grad)
    state_grad = seconds[7]
    later_grad = entering_3((device_decay, state_grad), "ctx", link, identity)[1]
    decay_grad = jnp.sum(later_grad * start_state, axis=(1, 2))
    firsts_grad = first_back(tuple(seconds[:7]) + (decay_grad, later_grad))
    edge_back = passed_along(firsts_grad[1], "ctx", -1)
    projected_grad = firsts_grad[0].reshape(rows_here, DPROJ)
    projected_grad = projected_grad.at[rows_here - (CONVK - 1) :, DI : DI + CH].add(edge_back)
    projected_low = projected_grad.astype(jnp.bfloat16)
    columns = normed_low
    in_weight_grad = lax.psum_scatter(
        lax.dot_general(
            columns, projected_low, (((0,), (0,)), ((), ())), preferred_element_type=jnp.float32
        ),
        ("fsdp", "ctx"),
        scatter_dimension=0,
        tiled=True,
    )
    normed_grad = lax.dot_general(
        projected_low, back_in, (((1,), (1,)), ((), ())), preferred_element_type=jnp.float32
    )
    input_part, norm_grad = norm_back(normed_grad)
    input_grad = cot32 + input_part
    summed = lax.psum(
        (
            norm_grad,
            firsts_grad[2],
            firsts_grad[3],
            firsts_grad[4],
            firsts_grad[5],
            seconds[8],
            seconds[9],
        ),
        ("fsdp", "ctx"),
    )
    return (
        output,
        input_grad,
        in_weight_grad,
        out_weight_grad,
        summed[0],
        summed[1],
        summed[2],
        summed[3],
        summed[4],
        summed[5],
        summed[6],
    )


def solution(mesh):
    return jax.shard_map(
        local,
        mesh=mesh,
        in_specs=(
            P(("fsdp", "ctx"), None),
            P(("fsdp", "ctx")),
            P(("fsdp", "ctx")),
            P(("fsdp", "ctx"), None),
            P(),
            P(("fsdp", "ctx"), None),
            P(),
            P(),
            P(),
            P(),
            P(),
            P(),
            P(("fsdp", "ctx"), None),
        ),
        out_specs=(
            P(("fsdp", "ctx"), None),
            P(("fsdp", "ctx"), None),
            P(("fsdp", "ctx"), None),
            P(("fsdp", "ctx"), None),
            P(),
            P(),
            P(),
            P(),
            P(),
            P(),
            P(),
        ),
        check_vma=False,
    )
```

profile of v0, /device:TPU:0, one launch (start us, length us, event | category | flops | bytes accessed | tf_op | source)
XLA Modules:
  0.0 868.7 jit_solution(12553991407036626769)
XLA Ops:
  13.8 79.8 %all-gather.8.cloned.1.call-done = bf16[1024,4384]{1,0:T(8,128)(2,1)} async-done(((bf16[32,4384]{1,0:T(8,128)(2,1)}), bf16[1024,4384]{1,0:T(8,128)(2,1)}) %all-gather.8.cloned.1.call-update) | async-done | bytes 8978448 | tf_op jit(solution)/shard_map/all_gather | solution.py:211
  93.6 17.6 %fusion.53 = f32[1024,4384]{0,1:T(8,128)} fusion(bf16[1024,4384]{1,0:T(8,128)(2,1)} %all-gather.8.cloned.1.call-done, bf16[1024,1024]{1,0:T(8,128)(2,1)} %param.23, f32[1024]{0:T(1024)} %param.27, f32[1024]{0:T(1024)S(1)} %fusion.87), kind=kOutput, calls=%fused_computation.128 | convolution fusion | flops 9198108672 | bytes 29040640 | tf_op jit(solution)/shard_map/dot_general | solution.py:222
  111.2 22.6 %reshape.267 = f32[4,256,4384]{1,0,2:T(4,128)} reshape(f32[1024,4384]{0,1:T(8,128)} %fusion.53) | data formatting | bytes 35913728 | tf_op jit(solution)/shard_map/reshape | solution.py:249
  150.8 9.6 %slice.143 = f32[4,256,2304]{1,0,2:T(4,128)} slice(f32[4,256,4384]{1,0,2:T(4,128)} %reshape.267), slice={[0:4], [0:256], [2048:4352]} | slice | bytes 18874368 | tf_op jit(solution)/shard_map/jvp()/slice | solution.py:122
  164.3 9.2 %copy.133 = f32[4,256,2304]{1,2,0:T(8,128)} copy(f32[4,256,2304]{1,0,2:T(4,128)} %slice.143) | data formatting | bytes 18874368
  176.6 23.9 %fusion.105 = (bf16[4,256,2304]{1,2,0:T(8,128)(2,1)}, f32[4,256,2304]{1,2,0:T(8,128)S(1)}, f32[4,256,2304]{1,2,0:T(8,128)}) fusion(f32[4,256,2304]{1,2,0:T(8,128)} %copy.133, f32[2304]{0:T(1024)S(1)} %get-tuple-element.473, f32[4,3,2304]{1,2,0:T(8,128)} %copy.78, f32[2304]{0:T(1024)S(1)} %get-tuple-element.474, f32[2304]{0:T(1024)S(1)} %get-tuple-element.472, ...), kind=kLoop, calls=%fused_computation.215 | loop fusion | flops 37748736 | bytes 33186816 | tf_op jit(solution)/shard_map/convert.3
  223.6 10.0 %copy.85 = f32[4,256,2048]{2,1,0:T(8,128)} copy(f32[4,256,2048]{1,0,2:T(4,128)} %slice.157) | data formatting | bytes 16777216 | tf_op jit(solution)/shard_map/jvp()/slice | solution.py:121
  234.0 11.0 %multiply_convert_fusion = bf16[4,32,256,256]{3,2,1,0:T(8,128)(2,1)} fusion(f32[4,32,256]{2,1,0:T(8,128)S(1)} %copy-done.30, f32[4,32,256]{2,1,0:T(8,128)S(1)} %fusion.65, f32[4,256,256]{2,1,0:T(8,128)S(1)} %fusion.109, pred[256,256]{1,0:T(8,128)(4,1)S(1)} %convert_compare_fusion), kind=kLoop, calls=%fused_computation.20 | loop fusion | flops 50331648 | bytes 18153472 | tf_op jit(solution)/shard_map/jvp()/convert_element_type | solution.py:68
  254.5 19.8 %while.63 = (s32[]{:T(128)}, f32[32,64,128]{2,1,0:T(8,128)S(1)}, f32[4,32,64,128]{3,2,1,0:T(8,128)}, f32[4,32,1,1]{1,3,2,0:T(1,128)}, f32[4,32]{1,0:T(4,128)S(1)...) while((s32[]{:T(128)}, f32[32,64,128]{2,1,0:T(8,128)S(1)}, f32[4,32,64,128]{3,2,1,0:T(8,128)}, ...), condition=%wide.region_4.5_spmd, body=%wide.region_3.4_spmd.sunk | while | flops 1048578 | bytes 5245549 | solution.py:181
  278.9 20.7 %multiply_reduce_fusion.9 = (f32[4,256]{1,0:T(4,128)}, f32[4,256,32,64]{1,3,2,0:T(8,128)}) fusion(f32[4,256,2048]{1,0,2:T(4,128)} %slice.157, f32[4,256,32,64]{1,3,2,0:T(8,128)} %bitcast.314, f32[32]{0:T(128)S(1)} %copy-done.73, f32[4,256,32,64]{1,3,2,0:T(8,128)S(1)} %fusion.57, f32[4,256,32]{1,2,0:T(8,128)S(1)} %copy-done.31, ...), kind=kOutput, calls=%fused_computation.72 | convolution fusion | flops 1096809472 | bytes 54661248 | tf_op jit(solution)/shard_map/jvp(chqs,cshp->cqhp)/dot_general | solution.py:151
  299.7 16.2 %copy.129 = f32[4,256,32,64]{3,2,1,0:T(8,128)} copy(f32[4,256,32,64]{1,3,2,0:T(8,128)} %get-tuple-element.571) | data formatting | bytes 16777216 | tf_op jit(solution)/shard_map/jvp()/reshape | solution.py:186
  315.9 15.0 %reshape.289 = f32[1024,2048]{1,0:T(8,128)} reshape(f32[4,256,32,64]{3,2,1,0:T(8,128)} %copy.129) | data formatting | bytes 16777216 | tf_op jit(solution)/shard_map/jvp()/reshape | solution.py:186
  331.0 14.4 %multiply_reduce_fusion.6 = (f32[2048]{0:T(1024)}, f32[1024]{0:T(1024)S(1)}, f32[1024,2048]{1,0:T(8,128)}) fusion(f32[1024]{0:T(1024)S(1)} %rsqrt.21, f32[1024,2048]{1,0:T(8,128)} %reshape.289, f32[4,256,2048]{2,1,0:T(8,128)} %copy.85, f32[2048]{0:T(1024)} %param.34, bf16[2048,1024]{1,0:T(8,128)(2,1)} %all-gather.12.cloned.1.call-done, ...), kind=kOutput, calls=%fused_computation.67 | convolution fusion | flops 4321178624 | bytes 31485952 | tf_op jit(solution)/shard_map/dot_general | solution.py:299
  345.4 16.0 %multiply_convert_fusion.1 = (bf16[1024,2048]{1,0:T(8,128)(2,1)}, f32[1024,2048]{1,0:T(8,128)}, bf16[1024,2048]{1,0:T(8,128)(2,1)}) fusion(f32[1024]{0:T(1024)S(1)} %multiply_multiply_fusion.2, f32[1024,2048]{1,0:T(8,128)} %get-tuple-element.572, f32[2048]{0:T(1024)S(1)} %copy-done.65, f32[1024]{0:T(1024)S(1)} %rsqrt.21, f32[4,256,2048]{2,1,0:T(8,128)} %copy.85, ...), kind=kLoop, calls=%fused_computation.69 | loop fusion | flops 46137344 | bytes 41959424 | tf_op jit(solution)/shard_map/transpose(jvp())/convert_element_type | solution.py:184
  375.7 9.5 %fusion.20 = (f32[32]{0:T(128)}, f32[4,256,32]{1,2,0:T(8,128)}, bf16[4,256,32,64]{1,3,2,0:T(8,128)(2,1)S(1)}) fusion(f32[4,256,32,64]{1,3,2,0:T(8,128)} %bitcast.315, bf16[4,256,32,64]{1,0,3,2:T(4,128)(2,1)} %convert_element_type.122, f32[4,256,32,64]{1,3,2,0:T(8,128)} %copy-done.9, f32[4,256,32]{1,2,0:T(8,128)S(1)} %copy-done.32), kind=kLoop, calls=%fused_computation.58 | loop fusion | flops 14647264 | bytes 25428096 | tf_op jit(solution)/shard_map/transpose(jvp())/reduce_sum | solution.py:184
  391.1 19.6 %while.64 = (s32[]{:T(128)}, f32[32,64,128]{2,1,0:T(8,128)S(1)}, f32[4,32,64,128]{3,2,1,0:T(8,128)}, f32[4,32]{1,0:T(4,128)S(1)}, f32[4]{0:T(128)S(1)}, /*index=...) while((s32[]{:T(128)}, f32[32,64,128]{2,1,0:T(8,128)S(1)}, ...), condition=%wide.region_9.10_spmd.clone, body=%wide.region_7.9_spmd.clone.sunk | while | flops 1834980 | bytes 6292388 | solution.py:181
  420.0 28.5 %fusion.8 = (f32[4,32,256]{2,1,0:T(8,128)}, f32[4,32,256]{2,1,0:T(8,128)}, f32[4,32,256]{2,1,0:T(8,128)}, bf16[4,256,256]{2,1,0:T(8,128)(2,1)S(1)}) fusion(f32[4,32,256]{2,1,0:T(8,128)} %get-tuple-element.559, f32[4,32,256]{2,1,0:T(8,128)S(1)} %fusion.65, f32[4,256,256]{2,1,0:T(8,128)S(1)} %copy-done.21, pred[256,256]{1,0:T(8,128)(4,1)} %copy-done.38, ...), kind=kOutput, calls=%fused_computation.28 | convolution fusion | flops 1199210496 | bytes 10682368 | tf_op jit(solution)/shard_map/transpose(jvp(chqs,cshp->cqhp))/dot_general | solution.py:151
  448.5 8.8 %copy.103 = f32[4,256,2048]{1,2,0:T(8,128)} copy(f32[4,256,2048]{2,1,0:T(8,128)} %bitcast.313) | data formatting | bytes 16777216 | tf_op jit(solution)/shard_map/transpose(jvp())/reshape | solution.py:186
  469.3 8.9 %while.65 = (s32[]{:T(128)}, f32[32,64,128]{2,1,0:T(8,128)S(1)}, s32[]{:T(128)}, f32[4,32,64,128]{3,2,1,0:T(8,128)}, f32[4,32]{1,0:T(4,128)}, /*index=5*/s32[]{:T(128)}, s32[]{:T(128)}, s32[]{:T(128)}, s32[]{:T(128)}) while((s32[]{:T(128)}, f32[32,64,128]{2,1,0:T(8,128)S(1)}, s32[]{:T(128)}, f32[4,32,64,128]{3,2,1,0:T(8,128)}, ...), condition=%wide.region_11.12_spmd.clone, body=%wide.region_10.11_spmd.clone.sunk | while | flops 1048584 | bytes 3146279 | solution.py:62
  497.3 17.8 %fusion.19 = f32[4,256,32,64]{1,3,2,0:T(8,128)} fusion(f32[4,256,32,64]{1,3,2,0:T(8,128)} %get-tuple-element.574, f32[32]{0:T(128)S(1)} %copy-done.74, f32[4,256,32]{1,2,0:T(8,128)S(1)} %copy-done.27, bf16[4,32,256,256]{3,2,1,0:T(8,128)(2,1)} %multiply_convert_fusion, bf16[4,32,64,256]{3,0,2,1:T(4,128)(2,1)} %bitcast.311, ...), kind=kOutput, calls=%fused_computation.57 | convolution fusion | flops 1084227584 | bytes 42074240 | tf_op jit(solution)/shard_map/transpose(jvp(chqs,cshp->cqhp))/dot_general | solution.py:151
  515.1 29.4 %multiply_reduce_fusion.4 = (f32[2304]{0:T(1024)}, f32[2304]{0:T(1024)S(1)}, f32[2304]{0:T(1024)}, f32[2304]{0:T(1024)}, f32[2304]{0:T(1024)}, /*index=5*/f32[4,256,2304]{1,2,0:T(8,128)}) fusion(f32[4,256,2304]{1,2,0:T(8,128)} %copy.133, f32[4,3,2304]{1,2,0:T(8,128)} %copy.78, f32[4,256,2304]{1,0,2:T(4,128)} %slice.143, ...), kind=kLoop, calls=%fused_computation.47 | loop fusion | flops 54252288 | bytes 47342592 | tf_op jit(solution)/shard_map/transpose(jvp())/reduce_sum | solution.py:132
  544.6 11.5 %broadcast_multiply_fusion = (f32[4,256,2304]{1,2,0:T(8,128)S(1)}, f32[4,256,2304]{1,2,0:T(8,128)S(1)}, f32[4,256,2304]{1,2,0:T(8,128)}, f32[4,256,2304]{1,2,0:T(8,128)}) fusion(f32[4,256,2304]{1,2,0:T(8,128)} %get-tuple-element.534, f32[2304]{0:T(1024)S(1)} %copy-done.45, f32[2304]{0:T(1024)S(1)} %copy-done.41, f32[2304]{0:T(1024)S(1)} %copy-done.43, ...), kind=kLoop, calls=%fused_computation.85 | loop fusion | flops 9437184 | bytes 47222784 | tf_op jit(solution)/shard_map/transpose(jvp())/mul | solution.py:132
  556.1 12.0 %add_multiply_fusion = f32[4,3,2304]{1,2,0:T(8,128)S(1)} fusion(f32[4,256,2304]{1,2,0:T(8,128)S(1)} %get-tuple-element.549, f32[4,256,2304]{1,2,0:T(8,128)} %get-tuple-element.550, f32[4,256,2304]{1,2,0:T(8,128)} %get-tuple-element.551, f32[4,256,2304]{1,2,0:T(8,128)S(1)} %get-tuple-element.548, f32[4]{0:T(128)S(1)} %copy-done.60), kind=kLoop, calls=%fused_computation.84 | loop fusion | flops 110592 | bytes 37859344 | tf_op jit(solution)/shard_map/transpose(jvp())/mul | solution.py:126
  577.8 20.8 %pad_add_fusion.1 = f32[4,259,2304]{1,2,0:T(8,128)} fusion(f32[4,256,2304]{1,2,0:T(8,128)} %copy-done.4, f32[4,256,2304]{1,2,0:T(8,128)} %get-tuple-element.550, f32[4,256,2304]{1,2,0:T(8,128)} %get-tuple-element.551, f32[4,256,2304]{1,2,0:T(8,128)} %copy-done.3), kind=kLoop, calls=%fused_computation.35 | loop fusion | flops 7160832 | bytes 47296512 | tf_op jit(solution)/shard_map/transpose(jvp())/add_any | solution.py:132
  598.5 12.3 %slice_add_fusion = f32[4,256,2304]{1,2,0:T(8,128)} fusion(f32[4,259,2304]{1,2,0:T(8,128)} %pad_add_fusion.1, f32[3,3,2304]{1,2,0:T(8,128)S(1)} %slice-done.6), kind=kLoop, calls=%fused_computation.43 | loop fusion | flops 2359296 | bytes 18957312 | tf_op jit(solution)/shard_map/transpose(jvp())/add_any | solution.py:126
  610.8 12.1 %pad_add_fusion = f32[4,256,4384]{1,2,0:T(8,128)} fusion(f32[4,256,2048]{1,2,0:T(8,128)} %copy.103, f32[4,256,2304]{1,2,0:T(8,128)} %slice_add_fusion, f32[4,256,32]{1,2,0:T(8,128)} %get-tuple-element.533), kind=kLoop, calls=%fused_computation.26 | loop fusion | flops 8978432 | bytes 35913728 | tf_op jit(solution)/shard_map/transpose(jvp())/add_any | solution.py:121
  622.9 18.3 %copy.104 = f32[4,256,4384]{2,1,0:T(8,128)} copy(f32[4,256,4384]{1,2,0:T(8,128)} %pad_add_fusion) | data formatting | bytes 35913728 | tf_op jit(solution)/shard_map/transpose(jvp())/add_any | solution.py:121
  644.0 17.9 %fusion.27 = f32[1024,4384]{1,0:T(8,128)} fusion(f32[1024,4384]{1,0:T(8,128)} %scatter-add.4, bf16[1024,1024]{1,0:T(8,128)(2,1)S(1)} %copy-done.13, f32[1024]{0:T(1024)S(1)} %copy-done.37, f32[1024]{0:T(1024)S(1)} %copy-done.36), kind=kOutput, calls=%fused_computation.89 | convolution fusion | flops 9202597888 | bytes 38019072 | tf_op jit(solution)/shard_map/dot_general | solution.py:324
  662.6 9.3 %fusion.35 = bf16[1024,1024]{1,0:T(8,128)(2,1)} fusion(bf16[1024,1024]{1,0:T(8,128)(2,1)S(1)} %copy-done.13, bf16[1024,2048]{1,0:T(8,128)(2,1)} %get-tuple-element.547, bf16[2048,1024]{1,0:T(8,128)(2,1)} %all-gather.12.cloned.1.call-done, f32[1024]{0:T(1024)S(1)} %copy-done.62), kind=kOutput, calls=%fused_computation.97 | convolution fusion | flops 4299161600 | bytes 12587008 | tf_op jit(solution)/shard_map/dot_general | solution.py:290
  672.1 18.4 %fusion.32 = (f32[1024]{0:T(1024)S(1)}, f32[1024]{0:T(1024)S(1)}, f32[1024,1024]{1,0:T(8,128)}) fusion(bf16[1024,1024]{1,0:T(8,128)(2,1)S(1)} %copy-done.13, f32[1024]{0:T(1024)S(1)} %copy-done.36, f32[1024]{0:T(1024)S(1)} %copy-done.37, bf16[1024,4384]{1,0:T(8,128)(2,1)} %all-gather.8.cloned.1.call-done, f32[1024,4384]{1,0:T(8,128)} %scatter-add.4), kind=kOutput, calls=%fused_computation.94 | convolution fusion | flops 9205741568 | bytes 33243136 | tf_op jit(solution)/shard_map/dot_general | solution.py:331
  690.6 43.5 %all-reduce.24 = (f32[1024]{0:T(1024)}, f32[4,2304]{1,0:T(4,128)}, f32[2304]{0:T(1024)}, f32[32]{0:T(128)}, f32[32]{0:T(128)}, /*index=5*/f32[32]{0:T(128)}, f32[2048]{0:T(1024)}) all-reduce(f32[1024]{0:T(1024)S(1)} %get-tuple-element.462, f32[4,2304]{1,0:T(4,128)S(1)} %pad_add_fusion.2, ...), channel_id=1, replica_groups=mesh['fsdp'=8,'ctx'=4] {'fsdp','ctx'}, use_global_device_ids=true, to_apply=%region_28.29 | all-reduce | flops 14688 | bytes 117504 | tf_op jit(solution)/shard_map/psum | solution.py:336
  739.0 122.6 %reduce-scatter.3.cloned.1.call-done = f32[32,4384]{1,0:T(8,128)} async-done(((f32[1024,4384]{1,0:T(8,128)}), f32[32,4384]{1,0:T(8,128)}) %reduce-scatter.3.cloned.1.call-update) | async-done | bytes 561168 | tf_op jit(solution)/shard_map/reduce_scatter | solution.py:323
  (351 shorter events, 193.5 us)
Async XLA Ops:
  7.2 86.4 %all-gather.8.cloned.1.call-start = ((), (), s32[]{:S(2)}) async-start(), calls=%async_computation.2 | async-start | bytes 9461760 | tf_op jit(solution)/shard_map/all_gather | solution.py:211
  7.9 243.8 %all-gather.10.cloned.1.call-start = ((), (), s32[]{:S(2)}) async-start(), calls=%async_computation.3 | async-start | bytes 2621440 | tf_op jit(solution)/shard_map/all_gather | solution.py:28
  8.6 452.9 %copy-start.61 = (f32[1024]{0:T(1024)}, f32[1024]{0:T(1024)S(1)}, u32[]{:S(2)}) copy-start(f32[1024]{0:T(1024)S(1)} %convert_element_type.107) | copy-start | bytes 12292
  8.7 128.2 %copy-start.54 = (f32[4,256]{1,0:T(4,128)}, f32[4,256]{1,0:T(4,128)S(1)}, u32[]{:S(2)}) copy-start(f32[4,256]{1,0:T(4,128)S(1)} %mul.772) | copy-start | bytes 12292
  11.0 165.5 %copy-start.40 = (f32[2304]{0:T(1024)}, f32[2304]{0:T(1024)S(1)}, u32[]{:S(2)}) copy-start(f32[2304]{0:T(1024)S(1)} %get-tuple-element.471) | copy-start | bytes 27652
  11.0 165.5 %copy-start.42 = (f32[2304]{0:T(1024)}, f32[2304]{0:T(1024)S(1)}, u32[]{:S(2)}) copy-start(f32[2304]{0:T(1024)S(1)} %get-tuple-element.472) | copy-start | bytes 27652
  11.0 165.5 %copy-start.44 = (f32[2304]{0:T(1024)}, f32[2304]{0:T(1024)S(1)}, u32[]{:S(2)}) copy-start(f32[2304]{0:T(1024)S(1)} %get-tuple-element.473) | copy-start | bytes 27652
  11.0 165.5 %copy-start.46 = (f32[2304]{0:T(1024)}, f32[2304]{0:T(1024)S(1)}, u32[]{:S(2)}) copy-start(f32[2304]{0:T(1024)S(1)} %get-tuple-element.474) | copy-start | bytes 27652
  11.7 124.6 %copy-start.92 = (f32[32]{0:T(128)}, f32[32]{0:T(128)S(1)}, u32[]{:S(2)}) copy-start(f32[32]{0:T(128)S(1)} %exponential_negate_fusion) | copy-start | bytes 388
  13.8 97.4 %copy-start.57 = (f32[1024]{0:T(1024)}, f32[1024]{0:T(1024)S(1)}, u32[]{:S(2)}) copy-start(f32[1024]{0:T(1024)S(1)} %fusion.34) | copy-start | bytes 12292
  13.8 97.4 %copy-start.35 = (f32[1024]{0:T(1024)}, f32[1024]{0:T(1024)S(1)}, u32[]{:S(2)}) copy-start(f32[1024]{0:T(1024)S(1)} %fusion.87) | copy-start | bytes 12292
  111.2 25.1 %copy-start.78 = (f32[32]{0:T(128)S(1)}, f32[32]{0:T(128)}, u32[]{:S(2)}) copy-start(f32[32]{0:T(128)} %param.31) | copy-start | bytes 388
  136.4 24.1 %copy-start.28 = (f32[4,256,32]{1,0,2:T(4,128)}, f32[4,256,32]{1,0,2:T(4,128)S(1)}, u32[]{:S(2)}) copy-start(f32[4,256,32]{1,0,2:T(4,128)S(1)} %slice.151) | copy-start | bytes 393220
  136.9 23.5 %copy-start.48 = (f32[4,32]{1,0:T(4,128)}, f32[4,32]{1,0:T(4,128)S(1)}, u32[]{:S(2)}) copy-start(f32[4,32]{1,0:T(4,128)S(1)} %slice_reduce_fusion) | copy-start | bytes 1540
  137.7 62.7 %copy-start.26 = (f32[4,256,32]{1,2,0:T(8,128)}, f32[4,256,32]{1,2,0:T(8,128)S(1)}, u32[]{:S(2)}) copy-start(f32[4,256,32]{1,2,0:T(8,128)S(1)} %get-tuple-element.560) | copy-start | bytes 393220
  138.1 35.4 %collective-permute-start = (f32[3,2304]{1,0:T(4,128)S(1)}, f32[3,2304]{1,0:T(4,128)S(1)}, u32[]{:S(2)}, u32[]{:S(2)}) collective-permute-start(f32[3,2304]{1,0:T(4,128)S(1)} %copy.73), channel_id=1, source_target_pairs={{0,1},{1,2},{2,3},{4,5},{5,6},{6,7},{8,9},{9,10},{10,11},{12,13},{... | collective-permute-start | bytes 82952 | tf_op jit(solution)/shard_map/ppermute | solution.py:22
  143.6 74.0 %copy-start.66 = (f32[1,32]{1,0:T(1,128)}, f32[1,32]{1,0:T(1,128)S(1)}, u32[]{:S(2)}) copy-start(f32[1,32]{1,0:T(1,128)S(1)} %get-tuple-element.537) | copy-start | bytes 388
  208.3 122.7 %all-gather.12.cloned.1.call-start = ((), (), s32[]{:S(2)}) async-start(), calls=%async_computation.4 | async-start | bytes 4325376 | tf_op jit(solution)/shard_map/all_gather | solution.py:212
  209.0 260.3 %all-gather.14.cloned.1.call-start = ((), (), s32[]{:S(2)}) async-start(), calls=%async_computation.7 | async-start | bytes 5242880 | tf_op jit(solution)/shard_map/all_gather | solution.py:49
  209.1 24.8 %copy-start.38 = (pred[256,256]{1,0:T(8,128)(4,1)}, pred[256,256]{1,0:T(8,128)(4,1)S(1)}, u32[]{:S(2)}) copy-start(pred[256,256]{1,0:T(8,128)(4,1)S(1)} %convert_compare_fusion) | copy-start | bytes 196612
  277.6 22.1 %copy-start.11 = (bf16[4,32,64,128]{3,2,1,0:T(8,128)(2,1)}, bf16[4,32,64,128]{3,2,1,0:T(8,128)(2,1)S(1)}, u32[]{:S(2)}) copy-start(bf16[4,32,64,128]{3,2,1,0:T(8,128)(2,1)S(1)} %convert_element_type.116) | copy-start | bytes 6291460
  391.1 28.9 %copy-start.21 = (f32[4,256,256]{2,1,0:T(8,128)S(1)}, f32[4,256,256]{2,1,0:T(8,128)}, u32[]{:S(2)}) copy-start(f32[4,256,256]{2,1,0:T(8,128)} %copy-done.20) | copy-start | bytes 3145732
  410.7 37.8 %copy-start.59 = (f32[4]{0:T(128)}, f32[4]{0:T(128)S(1)}, u32[]{:S(2)}) copy-start(f32[4]{0:T(128)S(1)} %get-tuple-element.867) | copy-start | bytes 52
  410.7 37.8 %copy-start.71 = (f32[4,32]{1,0:T(4,128)}, f32[4,32]{1,0:T(4,128)S(1)}, u32[]{:S(2)}) copy-start(f32[4,32]{1,0:T(4,128)S(1)} %get-tuple-element.405) | copy-start | bytes 1540
  411.7 327.3 %reduce-scatter.5.cloned.1.call-start = ((), (), s32[]{:S(2)}) async-start(), calls=%async_computation.6 | async-start | bytes 8650752 | tf_op jit(solution)/shard_map/reduce_scatter | solution.py:305
  469.2 392.4 %reduce-scatter.3.cloned.1.call-start = ((), (), s32[]{:S(2)}) async-start(), calls=%async_computation.5 | async-start | bytes 18923520 | tf_op jit(solution)/shard_map/reduce_scatter | solution.py:323
  515.1 29.4 %copy-start.41 = (f32[2304]{0:T(1024)S(1)}, f32[2304]{0:T(1024)}, u32[]{:S(2)}) copy-start(f32[2304]{0:T(1024)} %copy-done.40) | copy-start | bytes 27652
  515.1 29.4 %copy-start.43 = (f32[2304]{0:T(1024)S(1)}, f32[2304]{0:T(1024)}, u32[]{:S(2)}) copy-start(f32[2304]{0:T(1024)} %copy-done.42) | copy-start | bytes 27652
  515.1 29.4 %copy-start.45 = (f32[2304]{0:T(1024)S(1)}, f32[2304]{0:T(1024)}, u32[]{:S(2)}) copy-start(f32[2304]{0:T(1024)} %copy-done.44) | copy-start | bytes 27652
  515.1 29.4 %copy-start.47 = (f32[2304]{0:T(1024)S(1)}, f32[2304]{0:T(1024)}, u32[]{:S(2)}) copy-start(f32[2304]{0:T(1024)} %copy-done.46) | copy-start | bytes 27652
  573.6 67.6 %collective-permute-start.1 = (f32[3,2304]{1,0:T(4,128)}, f32[3,2304]{1,0:T(4,128)}, u32[]{:S(2)}, u32[]{:S(2)}) collective-permute-start(f32[3,2304]{1,0:T(4,128)} %copy.105), channel_id=1, source_target_pairs={{1,0},{2,1},{3,2},{5,4},{6,5},{7,6},{9,8},{10,9},{11,10},{13,12},{... | collective-permute-start | bytes 82952 | tf_op jit(solution)/shard_map/ppermute | solution.py:22
  672.1 62.0 %copy-start.58 = (f32[1024]{0:T(1024)S(1)}, f32[1024]{0:T(1024)}, u32[]{:S(2)}) copy-start(f32[1024]{0:T(1024)} %copy-done.57) | copy-start | bytes 12292
  (77 other events, 676.0 us)
Sparse Core Ops, SparseCore 0:
  10.8 82.6 all-gather.7
  208.4 21.1 all-gather.9
  232.4 61.7 all-gather.11
  411.8 36.0 all-gather.13
  469.3 148.0 reduce-scatter.4
  662.0 199.5 reduce-scatter.2
where the time goes:
time: 879 us; the launch traced here: 869 us
  other arithmetic  222 us (25%)
  waiting for transfers between devices  204 us (23%)
  local copies, waits for them, and re-layouts  192 us (22%)
  matrix products  174 us (20%)
  blocking collectives  57.1 us (6%)
  between operations  15.6 us (2%)
    reduce_scatter x1, waiting for transfers between devices, local(): lax.psum_scatter(lax.dot_general(columns, projected_low, (((0,), (0,)), (...  123 us
    all_gather x1, waiting for transfers between devices, local(): lax.all_gather(in_weight, ('fsdp', 'ctx'), axis=0, tiled=True)  79.8 us
    dot_general x3, matrix products, first_section(): local_out = jnp.einsum('chqs,cshp->cqhp', mixing, values_low)  67 us
    psum x1, blocking collectives, local(): lax.psum((norm_grad, firsts_grad[2], firsts_grad[3], firsts_grad[4], firs...  43.5 us
    reshape x2, local copies, waits for them, and re-layouts, second_section(): ssd_out.reshape(row_count, DI) * jax.nn.silu(gate_in.reshape(row_count, DI))  31.2 us
    reduce_sum x1, other arithmetic, first_section(): conv_weight[offset] * padded[:, offset:offset + width]  29.4 us
    another operation x1, other arithmetic  23.9 us
    reshape x1, local copies, waits for them, and re-layouts, local(): projected.reshape(blocks, Q, DPROJ)  22.6 us
  transfers between devices with their start and end apart: 8, of which 2 were waited for; matrix products, arithmetic and copies ran while one was open for 49% of the time, Pallas kernels for 0%

commit v1 on v0

v1 whole, which is shorter than its diff:
```python
import jax
import jax.numpy as jnp
from jax import lax
from jax.experimental import pallas as pl
from jax.experimental.pallas import tpu as pltpu
from jax.sharding import PartitionSpec as P

DI = 2048
HEADS = 32
P_SIZE = 64
N = 128
CONVK = 4
Q = 256
CH = 2304
DPROJ = 4384
UW = CH + 128
GW = 256
GROUPS = DI // GW
HALF = Q // 2

F32 = jnp.float32
BF16 = jnp.bfloat16
LOG2E = 1.4426950408889634
epsilon = 1e-05


def nn(a, b):
    return lax.dot_general(a, b, (((1,), (0,)), ((), ())), preferred_element_type=F32)


def nt(a, b):
    return lax.dot_general(a, b, (((1,), (1,)), ((), ())), preferred_element_type=F32)


def sigmoid(x):
    return 0.5 * jnp.tanh(0.5 * x) + 0.5


def softplus(x):
    e = jnp.exp(-jnp.abs(x))
    w = 1.0 + e
    d = w - 1.0
    return jnp.maximum(x, 0.0) + jnp.where(d == 0.0, e, jnp.log(w) * (e / jnp.where(d == 0.0, 1.0, d)))


def rows_of(shape):
    return lax.broadcasted_iota(jnp.int32, shape, 0)


def lanes_of(shape):
    return lax.broadcasted_iota(jnp.int32, shape, 1)


def split3(x):
    a = x.astype(BF16)
    r = x - a.astype(F32)
    b = r.astype(BF16)
    return a, b, (r - b.astype(F32)).astype(BF16)


def ordered_sum(triangle, x):
    a, b, c = split3(x)
    return nn(triangle, c) + nn(triangle, b) + nn(triangle, a)


def spread(x, out):
    out[0] = x
    for g in range(1, GROUPS):
        out[g] = pltpu.roll(x, 128 - 4 * g, 1)


def spread_rows(x, out):
    for g in range(GROUPS):
        out[g, 0:4] = x[4 * g : 4 * g + 4]


def head_lanes(x, i):
    return jnp.broadcast_to(x[:, i : i + 1], (x.shape[0], 128))


def pick_heads(g):
    shape = (GW, 128)
    return jnp.where(
        lax.shift_right_logical(rows_of(shape), 6) + 4 * g == lanes_of(shape), 1.0, 0.0
    ).astype(BF16)


def forward_kernel(
    u_ref, halo_ref, valid_ref, keep_ref, cw_ref, cb_ref, sb_ref, dl_ref, skip_ref,
    val_ref, vp_ref, conv_ref, bc_ref, ssd_ref, ent_ref, log_ref, step_ref, cum_ref, fin_ref,
    xpad, logs, steps, logt, inter, state,
):
    c = pl.program_id(0)

    @pl.when(c == 0)
    def _():
        xpad[0:8, :] = halo_ref[:, :CH] * keep_ref[0, 0]
        state[...] = jnp.zeros_like(state)
        cum_ref[...] = jnp.zeros_like(cum_ref)

    @pl.when(c > 0)
    def _():
        xpad[0:8, :] = xpad[Q : Q + 8, :]

    xpad[8 : 8 + Q, :] = u_ref[:, :CH]
    raw = u_ref[:, CH:] + sb_ref[...]
    step = softplus(raw) * valid_ref[...]
    step = jnp.where(lanes_of(step.shape) < HEADS, step, 0.0)
    rate = -jnp.exp(dl_ref[...]) * LOG2E
    square = (Q, Q)
    causal = rows_of(square) >= lanes_of(square)
    logd = ordered_sum(jnp.where(causal, 1.0, 0.0).astype(BF16), step * rate)
    log_ref[...] = logd
    step_ref[...] = step
    spread(logd, logs)
    spread(step, steps)
    spread_rows(logd.T, logt)
    half = lanes_of((Q, 128)) < P_SIZE

    def convolved(cols):
        total = cb_ref[:, cols] + cw_ref[0:1, cols] * xpad[5 : 5 + Q, cols]
        for k in range(1, CONVK):
            total = total + cw_ref[k : k + 1, cols] * xpad[5 + k : 5 + k + Q, cols]
        return total

    conv_b = convolved(pl.ds(DI, N))
    conv_c = convolved(pl.ds(DI + N, N))
    conv_ref[:, DI : DI + N] = conv_b.astype(BF16)
    conv_ref[:, DI + N :] = conv_c.astype(BF16)
    act_b = conv_b * sigmoid(conv_b)
    act_c = conv_c * sigmoid(conv_c)
    low_b = act_b.astype(BF16)
    low_c = act_c.astype(BF16)
    bc_ref[:, :N] = low_b
    bc_ref[:, N:] = low_c
    turned_b = act_b.T.astype(BF16)
    inter[...] = jnp.where(causal, nt(low_c, low_b), 0.0)
    ent_ref[0] = state[...].astype(BF16)

    def group(g, unused):
        lg = logs[g]
        sg = steps[g]
        for j in range(2):
            cols = pl.ds(pl.multiple_of(g * GW + 128 * j, 128), 128)
            cv = convolved(cols)
            conv_ref[:, cols] = cv.astype(BF16)
            val = cv * sigmoid(cv)
            val_ref[:, cols] = val.astype(BF16)
            lb = [head_lanes(lg, 2 * j), head_lanes(lg, 2 * j + 1)]
            lp = jnp.where(half, lb[0], lb[1])
            sp = jnp.where(half, head_lanes(sg, 2 * j), head_lanes(sg, 2 * j + 1))
            vp = val * sp
            vp_ref[:, cols] = vp.astype(BF16)
            last = lp[Q - 1 : Q, :]
            weighted = (vp * jnp.exp2(last - lp)).astype(BF16)
            state[:, cols] = jnp.exp2(last) * state[:, cols] + nn(turned_b, weighted)
            cum_ref[c + 1, :, cols] = cum_ref[c, :, cols] + last
            v0 = jnp.where(half, vp, 0.0).astype(BF16)
            v1 = jnp.where(half, 0.0, vp).astype(BF16)
            top = []
            low = []
            for i in range(2):
                row = logt[g, 2 * j + i : 2 * j + i + 1]
                early, late = row[:, :HALF], row[:, HALF:]
                up, down = lb[i][:HALF], lb[i][HALF:]
                top.append((inter[:HALF, :HALF] * jnp.exp2(jnp.minimum(up - early, 0.0))).astype(BF16))
                low.append((inter[HALF:, :HALF] * jnp.exp2(jnp.minimum(down - early, 0.0))).astype(BF16))
                low.append((inter[HALF:, HALF:] * jnp.exp2(jnp.minimum(down - late, 0.0))).astype(BF16))
            skipped = skip_ref[:, cols] * val
            first = nn(jnp.concatenate(top, 1), jnp.concatenate([v0[:HALF], v1[:HALF]], 0))
            second = nn(jnp.concatenate(low, 1), jnp.concatenate([v0, v1], 0))
            ssd_ref[:HALF, cols] = (first + skipped[:HALF]).astype(BF16)
            ssd_ref[HALF:, cols] = (second + skipped[HALF:]).astype(BF16)
        return unused

    lax.fori_loop(0, GROUPS, group, 0)

    @pl.when(c == pl.num_programs(0) - 1)
    def _():
        fin_ref[:N, :] = state[...].astype(BF16)
        a, b, d = split3(cum_ref[c + 1, 0:1, :])
        shape = (16, DI)
        r = rows_of(shape)
        pick = jnp.where(r == 0, jnp.broadcast_to(a.astype(F32), shape), 0.0)
        pick = jnp.where(r == 1, jnp.broadcast_to(b.astype(F32), shape), pick)
        pick = jnp.where(r == 2, jnp.broadcast_to(d.astype(F32), shape), pick)
        pick = jnp.where(r == 3, keep_ref[0, 0], pick)
        fin_ref[N:, :] = pick.astype(BF16)


def decays_and_keeps(tail_ref, count):
    decays = []
    keeps = []
    for k in range(count):
        rows = tail_ref[k].astype(F32)
        decays.append(jnp.exp2(rows[0:1] + rows[1:2] + rows[2:3]))
        keeps.append(rows[3:4])
    return decays, keeps


def gate_kernel(
    pos_ref, keep_ref, all_ref, tail_ref, ssd_in, ent_ref, z_ref, val_ref, bc_ref, log_ref, cum_ref,
    tok_ref, cot_ref, valid_ref, ow_ref, gain_ref,
    out_ref, gated_ref, bg_ref, ds_ref, dz_ref, entt_ref, gnext_ref, gout_ref, dlp_ref, dc_ref, sums_ref,
    start, gstate, logs, ssd_s, mix_s, el_s, pe_s, gg_s, acc,
):
    i = pl.program_id(0)
    c = pl.num_programs(0) - 1 - i

    @pl.when(i == 0)
    def _():
        count = all_ref.shape[0]
        decays, keeps = decays_and_keeps(tail_ref, count)
        pos = pos_ref[0, 0]
        for k in range(count):
            factor = jnp.where(k < pos, keep_ref[0, 0], 0.0) * jnp.ones((1, DI), F32)
            for m in range(k + 1, count):
                factor = factor * jnp.where(m < pos, decays[m] * keeps[m], 1.0)
            term = factor * all_ref[k].astype(F32)
            start[...] = term if k == 0 else start[...] + term
        gstate[...] = jnp.zeros_like(gstate)
        sums_ref[...] = jnp.zeros_like(sums_ref)

    spread(log_ref[...], logs)
    low_c = bc_ref[:, N:]
    turned_c = low_c.astype(F32).T.astype(BF16)
    half = lanes_of((Q, 128)) < P_SIZE
    acc[...] = jnp.zeros_like(acc)

    def enter(g, unused):
        lg = logs[g]
        cols = pl.ds(pl.multiple_of(g * GW, GW), GW)
        entering = (
            ent_ref[0, :, cols].astype(F32) + jnp.exp2(cum_ref[c, 0:1, cols]) * start[:, cols]
        ).astype(BF16)
        entt_ref[0, :, cols] = entering
        part = nn(low_c, entering)
        for j in range(2):
            pc = pl.ds(pl.multiple_of(g * GW + 128 * j, 128), 128)
            el = jnp.exp2(jnp.where(half, head_lanes(lg, 2 * j), head_lanes(lg, 2 * j + 1)))
            pe = el * part[:, 128 * j : 128 * j + 128]
            el_s[:, pc] = el
            pe_s[:, pc] = pe
            ssd = ssd_in[:, pc].astype(F32) + pe
            z = z_ref[:, pc].astype(F32)
            mixed = ssd * (z * sigmoid(z))
            ssd_s[:, pc] = ssd
            mix_s[:, pc] = mixed
            acc[...] += mixed * mixed
        return unused

    lax.fori_loop(0, GROUPS, enter, 0)
    inv = lax.rsqrt(jnp.sum(acc[...], axis=1, keepdims=True) * (1.0 / DI) + epsilon)
    inv = jnp.broadcast_to(inv, (Q, 128))
    valid = valid_ref[...]
    valid8 = jnp.concatenate([valid] * (tok_ref.shape[1] // 128), 1)
    branch_grad = (cot_ref[...].astype(F32) * valid8).astype(BF16)
    bg_ref[...] = branch_grad
    acc[...] = jnp.zeros_like(acc)

    def gate(g, unused):
        cols = pl.ds(pl.multiple_of(g * GW, GW), GW)
        ggrad = nt(branch_grad, ow_ref[cols, :])
        for j in range(2):
            pc = pl.ds(pl.multiple_of(g * GW + 128 * j, 128), 128)
            hat = mix_s[:, pc] * inv
            gain = gain_ref[:, pc]
            mix_s[:, pc] = hat
            gated_ref[:, pc] = (hat * gain).astype(BF16)
            gg = ggrad[:, 128 * j : 128 * j + 128]
            both = gg * hat
            sums_ref[0:1, pc] += jnp.sum(both, axis=0, keepdims=True)
            acc[...] += both * gain
            gg_s[:, pc] = gg * gain
        return unused

    lax.fori_loop(0, GROUPS, gate, 0)
    mean = jnp.sum(acc[...], axis=1, keepdims=True) * (1.0 / DI)
    mean = jnp.broadcast_to(mean, (Q, 128))

    for n in range(tok_ref.shape[1] // 256):
        cols = slice(256 * n, 256 * n + 256)
        branch = nn(gated_ref[...], ow_ref[:, cols])
        out_ref[:, cols] = (tok_ref[:, cols].astype(F32) + valid8[:, :256] * branch).astype(BF16)

    acc[...] = jnp.zeros_like(acc)
    dc_ref[...] = jnp.zeros_like(dc_ref)

    def back(g, unused):
        cols = pl.ds(pl.multiple_of(g * GW, GW), GW)
        dparts = []
        prods = []
        for j in range(2):
            pc = pl.ds(pl.multiple_of(g * GW + 128 * j, 128), 128)
            dmixed = inv * (gg_s[:, pc] - mix_s[:, pc] * mean)
            z = z_ref[:, pc].astype(F32)
            s = sigmoid(z)
            ds = (dmixed * (z * s)).astype(BF16)
            ds_ref[:, pc] = ds
            dz_ref[:, pc] = (dmixed * ssd_s[:, pc] * (s * (1.0 + z * (1.0 - s)))).astype(BF16)
            ds = ds.astype(F32)
            sums_ref[1:2, pc] += jnp.sum(ds * val_ref[:, pc].astype(F32), axis=0, keepdims=True)
            dparts.append((ds * el_s[:, pc]).astype(BF16))
            prods.append((ds * pe_s[:, pc]).astype(BF16))
        dpart = jnp.concatenate(dparts, 1)
        acc[...] += nn(jnp.concatenate(prods, 1), pick_heads(g))
        dc_ref[...] += nt(dpart, entt_ref[0, :, cols])
        gnext_ref[0, :, cols] = gstate[:, cols].astype(BF16)
        total = cum_ref[c + 1, 0:1, cols] - cum_ref[c, 0:1, cols]
        gstate[:, cols] = nn(turned_c, dpart) + jnp.exp2(total) * gstate[:, cols]
        return unused

    lax.fori_loop(0, GROUPS, back, 0)
    dlp_ref[...] = acc[...]

    @pl.when(c == 0)
    def _():
        gout_ref[...] = gstate[...].astype(BF16)


def mixing_kernel(ds_ref, vp_ref, bc_ref, log_ref, dvp_ref, dbc_ref, dlt_ref, logs, logt, inter, dinter, rowsum, turned, colsum):
    logd = log_ref[...]
    spread(logd, logs)
    spread_rows(logd.T, logt)
    low_b = bc_ref[:, :N]
    low_c = bc_ref[:, N:]
    square = (Q, Q)
    causal = rows_of(square) <= lanes_of(square)
    inter[...] = jnp.where(causal, nt(low_b, low_c), 0.0)
    dinter[...] = jnp.zeros_like(dinter)
    half = lanes_of((Q, 128)) < P_SIZE
    lane = lanes_of((HALF, 128))

    def group(g, unused):
        lg = logs[g]
        first_col = jnp.zeros((HALF, 128), F32)
        second_col = jnp.zeros((HALF, 128), F32)
        for j in range(2):
            cols = pl.ds(pl.multiple_of(g * GW + 128 * j, 128), 128)
            vp = vp_ref[:, cols].astype(F32)
            ds = ds_ref[:, cols]
            wide = ds.astype(F32)
            first = []
            second = []
            outs = []
            for i in range(2):
                head = 2 * j + i
                own = half if i == 0 else jnp.logical_not(half)
                vm = jnp.where(own, vp, 0.0).astype(BF16)
                dsm = jnp.where(own, wide, 0.0).astype(BF16)
                outs.append(dsm)
                row = logt[g, head : head + 1]
                early, late = row[:, :HALF], row[:, HALF:]
                lb = head_lanes(lg, head)
                up, down = lb[:HALF], lb[HALF:]
                dup = nt(vm[:HALF], ds)
                ddown = nt(vm[HALF:], ds[HALF:])
                decay = jnp.exp2(jnp.minimum(early - up, 0.0))
                grad = dup[:, :HALF] * decay
                dinter[:HALF, :HALF] += grad
                part = inter[:HALF, :HALF]
                first.append((part * decay).astype(BF16))
                both = grad * part
                row_early = jnp.sum(both, axis=0, keepdims=True)
                col = both
                decay = jnp.exp2(jnp.minimum(late - up, 0.0))
                grad = dup[:, HALF:] * decay
                dinter[:HALF, HALF:] += grad
                part = inter[:HALF, HALF:]
                first.append((part * decay).astype(BF16))
                both = grad * part
                row_late = jnp.sum(both, axis=0, keepdims=True)
                col = jnp.sum(col + both, axis=1, keepdims=True)
                first_col = jnp.where(lane == head, col, first_col)
                decay = jnp.exp2(jnp.minimum(late - down, 0.0))
                grad = ddown * decay
                dinter[HALF:, HALF:] += grad
                part = inter[HALF:, HALF:]
                second.append((part * decay).astype(BF16))
                both = grad * part
                row_late = row_late + jnp.sum(both, axis=0, keepdims=True)
                col = jnp.sum(both, axis=1, keepdims=True)
                second_col = jnp.where(lane == head, col, second_col)
                rowsum[g, head : head + 1, :HALF] = row_early
                rowsum[g, head : head + 1, HALF:] = row_late
            dvp_ref[:HALF, cols] = nn(
                jnp.concatenate(first, 1), jnp.concatenate(outs, 0)
            ).astype(BF16)
            dvp_ref[HALF:, cols] = nn(
                jnp.concatenate(second, 1), jnp.concatenate([outs[0][HALF:], outs[1][HALF:]], 0)
            ).astype(BF16)
        colsum[g, :HALF] = first_col
        colsum[g, HALF:] = second_col
        return unused

    lax.fori_loop(0, GROUPS, group, 0)
    turned[...] = jnp.zeros_like(turned)
    for g in range(GROUPS):
        turned[4 * g : 4 * g + 4] = rowsum[g, 0:4]
    total = turned[...].T
    for g in range(GROUPS):
        total = total - (colsum[g] if g == 0 else pltpu.roll(colsum[g], 4 * g, 1))
    dlt_ref[...] = total
    masked = jnp.where(causal, dinter[...], 0.0)
    dbc_ref[:, :N] = nn(masked.astype(BF16), low_c)
    dbc_ref[:, N:] = nn(masked.T.astype(BF16), low_b)


def back_kernel(
    pos_ref, keep_ref, all_ref, tail_ref, gnext_ref, entt_ref, cum_ref, vp_ref, val_ref, dvp_ref, ds_ref, conv_ref,
    u_ref, halo_ref, bc_ref, log_ref, step_ref, valid_ref, dlp_ref, dlt_ref, dbc_ref, dc_ref,
    cw_ref, sb_ref, dl_ref, skip_ref,
    du_ref, last_ref, edge_ref, sums_ref, small_ref,
    gin, logs, steps, dpad, head, epad, dlw, dst, drow,
):
    i = pl.program_id(0)
    top = pl.num_programs(0)
    c = top - 1 - i

    @pl.when(i == 0)
    def _():
        count = all_ref.shape[0]
        decays, keeps = decays_and_keeps(tail_ref, count)
        pos = pos_ref[0, 0]
        for k in range(count):
            factor = jnp.where(k > pos, keeps[k], 0.0)
            for m in range(k):
                factor = factor * jnp.where(m > pos, decays[m] * keeps[m], 1.0)
            term = factor * all_ref[k].astype(F32)
            gin[...] = term if k == 0 else gin[...] + term
        head[...] = jnp.zeros_like(head)
        sums_ref[...] = jnp.zeros_like(sums_ref)
        small_ref[...] = jnp.zeros_like(small_ref)

    spread(log_ref[...], logs)
    spread(step_ref[...], steps)
    low_b = bc_ref[:, :N]
    half = lanes_of((Q, 128)) < P_SIZE
    dlw[...] = jnp.zeros_like(dlw)
    dst[...] = jnp.zeros_like(dst)
    drow[...] = jnp.zeros_like(drow)

    def conv_back(cols, dact):
        cv = conv_ref[:, cols].astype(F32)
        s = sigmoid(cv)
        dcv = dact * (s * (1.0 + cv * (1.0 - s)))
        dpad[:Q, cols] = dcv
        dpad[Q:, cols] = head[:, cols]
        head[:, cols] = dcv[:8]
        x = u_ref[:, cols]
        sums_ref[4:5, cols] += jnp.sum(dcv, axis=0, keepdims=True)
        total = None
        for j in range(CONVK):
            k = CONVK - 1 - j
            moved = dcv if j == 0 else dpad[j : j + Q, cols]
            sums_ref[k : k + 1, cols] += jnp.sum(moved * x, axis=0, keepdims=True)
            term = cw_ref[k : k + 1, cols] * moved
            total = term if total is None else total + term
        du_ref[:, cols] = total.astype(BF16)

        @pl.when(i == 0)
        def _():
            last_ref[:, cols] = total[Q - 8 :]

    def group(g, db):
        lg = logs[g]
        sg = steps[g]
        cols = pl.ds(pl.multiple_of(g * GW, GW), GW)
        done = cum_ref[c + 1, 0:1, cols]
        after = jnp.exp2(cum_ref[top, 0:1, cols] - done)
        grad = gnext_ref[0, :, cols].astype(F32) + after * gin[:, cols]
        low_g = grad.astype(BF16)
        decay = jnp.exp2(done - cum_ref[c, 0:1, cols])
        row = decay * jnp.sum(grad * entt_ref[0, :, cols].astype(F32), axis=0, keepdims=True)
        coarse = row.astype(BF16).astype(F32)
        r = rows_of((16, GW))
        two = jnp.where(r == 0, jnp.broadcast_to(coarse, (16, GW)), 0.0)
        two = jnp.where(r == 1, jnp.broadcast_to(row - coarse, (16, GW)), two)
        chosen = pick_heads(g)
        drow[...] += nn(two.astype(BF16), chosen)
        dweighted = nn(low_b, low_g)
        weights = []
        moves = []
        stepped = []
        dacts = []
        for j in range(2):
            pc = pl.ds(pl.multiple_of(g * GW + 128 * j, 128), 128)
            lp = jnp.where(half, head_lanes(lg, 2 * j), head_lanes(lg, 2 * j + 1))
            sp = jnp.where(half, head_lanes(sg, 2 * j), head_lanes(sg, 2 * j + 1))
            fade = jnp.exp2(lp[Q - 1 : Q, :] - lp)
            vp = vp_ref[:, pc].astype(F32)
            faded = dweighted[:, 128 * j : 128 * j + 128] * fade
            weights.append((vp * fade).astype(BF16))
            moves.append((faded * vp).astype(BF16))
            both = dvp_ref[:, pc].astype(F32) + faded
            stepped.append((both * val_ref[:, pc].astype(F32)).astype(BF16))
            dacts.append((pc, sp * both + skip_ref[:, pc] * ds_ref[:, pc].astype(F32)))
        dlw[...] += nn(jnp.concatenate(moves, 1), chosen)
        dst[...] += nn(jnp.concatenate(stepped, 1), chosen)
        for pc, dact in dacts:
            conv_back(pc, dact)
        return db + nt(jnp.concatenate(weights, 1), low_g)

    db = lax.fori_loop(0, GROUPS, group, dbc_ref[:, :N])
    conv_back(pl.ds(DI, N), db)
    conv_back(pl.ds(DI + N, N), dbc_ref[:, N:] + dc_ref[...])

    moved = dlw[...]
    at_last = jnp.sum(moved, axis=0, keepdims=True) + drow[0:1] + drow[1:2]
    dlog = dlp_ref[...] + dlt_ref[...] - moved
    dlog = dlog + jnp.where(rows_of(dlog.shape) == Q - 1, at_last, 0.0)
    square = (Q, Q)
    later = jnp.where(rows_of(square) <= lanes_of(square), 1.0, 0.0).astype(BF16)
    dsum = ordered_sum(later, dlog)
    rate = -jnp.exp(dl_ref[...])
    dstep = (dst[...] + dsum * rate) * valid_ref[...]
    raw = u_ref[:, CH:] + sb_ref[...]
    draw = dstep * (1.0 / (1.0 + jnp.exp(-raw)))
    draw = jnp.where(lanes_of(draw.shape) < HEADS, draw, 0.0)
    du_ref[:, CH:] = draw.astype(BF16)
    small_ref[0:1] += jnp.sum(draw, axis=0, keepdims=True)
    small_ref[1:2] += jnp.sum(dsum * step_ref[...], axis=0, keepdims=True) * rate

    @pl.when(c == 0)
    def _():
        epad[0:8, :] = jnp.zeros((8, CH), F32)
        epad[8:16, :] = head[...]
        x = halo_ref[:, :CH] * keep_ref[0, 0]
        total = jnp.zeros((8, CH), F32)
        for j in range(CONVK):
            k = CONVK - 1 - j
            moved = epad[j : j + 8, :]
            sums_ref[k : k + 1, :] += jnp.sum(moved * x, axis=0, keepdims=True)
            total = total + cw_ref[k : k + 1, :] * moved
        edge_ref[...] = total * keep_ref[0, 0]


def spec(block, index):
    return pl.BlockSpec(block, index)


def whole(shape):
    return pl.BlockSpec(shape, lambda *_: (0,) * len(shape))


def scalar():
    return pl.BlockSpec(memory_space=pltpu.SMEM)


def shaped(shape, kind):
    return jax.ShapeDtypeStruct(shape, kind)


def cost(flops, moved):
    return pl.CostEstimate(flops=int(flops), bytes_accessed=int(moved), transcendentals=0)


def params():
    return pltpu.CompilerParams(dimension_semantics=("arbitrary",), vmem_limit_bytes=60 * 1024 * 1024)


LINE = 4


def my_place():
    f = lax.axis_index("fsdp")
    t = lax.axis_index("ctx")
    return f // 2, f % 2, t // 2, t % 2


def device_at(z, y, x, core):
    return {"fsdp": z * 2 + y, "ctx": x * 2 + core}


def order_of(z, y, x, core):
    return (z * 2 + y) * 4 + x * 2 + core


def meet(more=()):
    z, y, x, core = my_place()
    barrier = pltpu.get_barrier_semaphore()
    fixed = [(z, y, x, 1 - core), (z, y, 1 - x, core), (z, 1 - y, x, core)] + list(more)
    for peer in fixed:
        pl.semaphore_signal(
            barrier, inc=1, device_id=device_at(*peer), device_id_type=pl.DeviceIdType.MESH
        )

    @pl.when(z > 0)
    def _():
        pl.semaphore_signal(
            barrier, inc=1, device_id=device_at(z - 1, y, x, core), device_id_type=pl.DeviceIdType.MESH
        )

    @pl.when(z < LINE - 1)
    def _():
        pl.semaphore_signal(
            barrier, inc=1, device_id=device_at(z + 1, y, x, core), device_id_type=pl.DeviceIdType.MESH
        )

    ends = jnp.where(z > 0, 1, 0) + jnp.where(z < LINE - 1, 1, 0)
    pl.semaphore_wait(barrier, len(fixed) + ends)


def send(src, dst, send_sem, recv_sem, peer):
    return pltpu.make_async_remote_copy(
        src_ref=src, dst_ref=dst, send_sem=send_sem, recv_sem=recv_sem,
        device_id=device_at(*peer), device_id_type=pl.DeviceIdType.MESH,
    )


class Gather:
    def __init__(self, own, out, recv, halves, twin, sent, here):
        self.own, self.out, self.rows = own, out, own.shape[0]
        self.recv, self.halves, self.twin, self.sent, self.here = recv, halves, twin, sent, here
        self.place = my_place()

    def block(self, z, y, x, core, half=None):
        size = self.rows if half is None else self.rows // 2
        start = order_of(z, y, x, core) * self.rows + (0 if half is None else half * size)
        return self.out.at[pl.ds(pl.multiple_of(start, 16), size)]

    def copy(self, origin, way, half=None, own=False):
        z, y, x, core = self.place
        oz, oy, ox = origin
        o = oz * 4 + oy * 2 + ox
        dst = self.block(oz, oy, ox, core, half)
        src = self.own if own else dst
        peer = {
            "up": (z + 1, y, x, core), "down": (z - 1, y, x, core), "x": (z, y, 1 - x, core),
            "y": (z, 1 - y, x, core), "twin": (z, y, x, 1 - core),
        }[way]
        sem = self.sent.at[("up", "down", "x", "y", "twin").index(way), o]
        if way == "twin":
            arrival = self.twin.at[o]
        elif half is not None:
            arrival = self.halves.at[half, o]
        else:
            arrival = self.recv.at[o]
        return send(src, dst, sem, arrival, peer)

    def arrived(self, origin, half=None):
        self.copy(origin, "x", half).wait_recv()

    def column(self, r):
        z = self.place[0]
        if r == 0:
            return [(None, z, True, True)]
        return [(z - r >= 0, z - r, True, False), (z + r < LINE, z + r, False, True)]

    def each(self, r, act):
        for valid, oz, below, above in self.column(r):
            if valid is None:
                act(oz, below, above)
            else:
                pl.when(valid)(lambda oz=oz, below=below, above=above: act(oz, below, above))

    def begin(self):
        z, y, x, core = self.place
        pltpu.make_async_copy(self.own, self.block(z, y, x, core), self.here).start()
        self.forward(0)

    def ways(self, oz, below, above, act):
        z = self.place[0]
        if below:
            pl.when(z < LINE - 1)(lambda: act("up"))
        if above:
            pl.when(z > 0)(lambda: act("down"))
        act("x")
        act("y")
        act("twin")

    def forward(self, r):
        z, y, x, core = self.place

        def act(oz, below, above):
            origin = (oz, y, x)
            if r:
                self.arrived(origin)
            self.ways(oz, below, above, lambda way: self.copy(origin, way, own=r == 0).start())

        self.each(r, act)

    def across(self, r):
        z, y, x, core = self.place

        def act(oz, below, above):
            self.arrived((oz, y, 1 - x))
            self.copy((oz, y, 1 - x), "y", 0).start()
            self.copy((oz, y, 1 - x), "twin").start()
            self.arrived((oz, 1 - y, x))
            self.copy((oz, 1 - y, x), "x", 1).start()
            self.copy((oz, 1 - y, x), "twin").start()

        self.each(r, act)

    def corner(self, r):
        z, y, x, core = self.place

        def act(oz, below, above):
            origin = (oz, 1 - y, 1 - x)
            self.arrived(origin, 0)
            self.arrived(origin, 1)
            self.copy(origin, "twin").start()

        self.each(r, act)

    def finish(self):
        z, y, x, core = self.place
        pltpu.make_async_copy(self.own, self.block(z, y, x, core), self.here).wait()
        for r in range(LINE):

            def act(oz, below, above, r=r):
                self.ways(oz, below, above, lambda way: self.copy((oz, y, x), way, own=r == 0).wait_send())
                self.copy((oz, y, 1 - x), "y", 0).wait_send()
                self.copy((oz, 1 - y, x), "x", 1).wait_send()
                for oy, ox in ((y, 1 - x), (1 - y, x), (1 - y, 1 - x)):
                    self.copy((oz, oy, ox), "twin").wait_send()
                for oy, ox in ((y, x), (y, 1 - x), (1 - y, x), (1 - y, 1 - x)):
                    self.copy((oz, oy, ox), "twin").wait_recv()

            self.each(r, act)

    def steps(self):
        return [
            self.begin,
            lambda: self.forward(1),
            lambda: self.across(0),
            lambda: self.forward(2),
            lambda: self.across(1),
            lambda: (self.forward(3), self.corner(0)),
            lambda: self.across(2),
            lambda: self.corner(1),
            lambda: self.across(3),
            lambda: (self.corner(2), self.corner(3)),
            self.finish,
        ]


def gather_scratch():
    dma = pltpu.SemaphoreType.DMA
    return [dma((16,)), dma((2, 16)), dma((16,)), dma((5, 16)), dma(())]


def gather_kernel(count, *refs):
    own, out, sems = refs[:count], refs[count : 2 * count], refs[2 * count :]
    meet()
    lists = [
        Gather(own[k], out[k], *sems[5 * k : 5 * k + 5]).steps() for k in range(count)
    ]
    length = len(lists[0])
    for at in range(length + 2 * (count - 1)):
        for k in range(count):
            if 0 <= at - 2 * k < length:
                lists[k][at - 2 * k]()


def gathered(arrays, number):
    count = len(arrays)
    anywhere = pl.BlockSpec(memory_space=pl.ANY)
    return pl.pallas_call(
        lambda *refs: gather_kernel(count, *refs),
        in_specs=[anywhere] * count,
        out_specs=[anywhere] * count,
        out_shape=[shaped((32 * a.shape[0], a.shape[1]), a.dtype) for a in arrays],
        scratch_shapes=gather_scratch() * count,
        compiler_params=pltpu.CompilerParams(collective_id=number, has_side_effects=True),
        name="gather",
    )(*arrays)


class Scatter:
    def __init__(self, parts, out, twin, got, kept, mixed_y, mixed_x, from_x, from_y, up, down, sems):
        self.parts, self.out = parts, out
        self.got, self.kept = got, kept
        self.mixed = (mixed_y, mixed_x)
        self.sides = (from_x, from_y)
        self.up, self.down = up, down
        self.twin_sent, self.twin_recv, self.sent, self.recv, self.line_sent, self.line_recv = sems
        self.place = my_place()
        self.rows = parts.shape[-2]

    def groups(self):
        z, y, x, core = self.place
        return [(1 - y, 1 - x), (y, 1 - x), (1 - y, x), (y, x)]

    def to_twin(self, k):
        z, y, x, core = self.place
        gy, gx = self.groups()[k]
        return send(
            self.parts.at[:, gy, gx, 1 - core], self.got.at[k], self.twin_sent.at[k], self.twin_recv.at[k],
            (z, y, x, 1 - core),
        )

    def begin(self):
        for k in range(4):
            self.to_twin(k).start()

    def both(self, k):
        z, y, x, core = self.place
        gy, gx = self.groups()[k]
        self.to_twin(k).wait_recv()
        for b in range(LINE):
            total = self.parts[b, gy, gx, core].astype(F32) + self.got[k, b].astype(F32)
            self.kept[k, b] = total.astype(BF16)

    def corner_copy(self, half):
        z, y, x, core = self.place
        size = self.rows // 2
        src = self.kept.at[0, :, pl.ds(half * size, size)]
        peer = (z, 1 - y, x, core) if half == 0 else (z, y, 1 - x, core)
        return send(src, self.mixed[half], self.sent.at[half], self.recv.at[half], peer)

    def side_copy(self, k):
        z, y, x, core = self.place
        peer = (z, y, 1 - x, core) if k == 1 else (z, 1 - y, x, core)
        return send(self.kept.at[k], self.sides[k - 1], self.sent.at[1 + k], self.recv.at[1 + k], peer)

    def corners(self):
        self.both(0)
        self.corner_copy(0).start()
        self.corner_copy(1).start()
        self.both(1)
        self.both(2)
        self.both(3)

    def sides_out(self):
        size = self.rows // 2
        for half, k in ((0, 1), (1, 2)):
            self.corner_copy(half).wait_recv()
            rows = slice(half * size, half * size + size)
            for b in range(LINE):
                total = self.kept[k, b, rows].astype(F32) + self.mixed[half][b].astype(F32)
                self.kept[k, b, rows] = total.astype(BF16)
            self.side_copy(k).start()

    def sides_in(self):
        self.side_copy(1).wait_recv()
        self.side_copy(2).wait_recv()
        for b in range(LINE):
            total = self.kept[3, b].astype(F32) + self.sides[0][b].astype(F32) + self.sides[1][b].astype(F32)
            self.kept[3, b] = total.astype(BF16)

    def line_copy(self, oz, way):
        z, y, x, core = self.place
        buffer = self.up if way == 0 else self.down
        peer = (z + 1, y, x, core) if way == 0 else (z - 1, y, x, core)
        return send(
            self.kept.at[3, oz], buffer.at[oz], self.line_sent.at[way, oz], self.line_recv.at[way, oz], peer
        )

    def line(self, r):
        z = self.place[0]

        def upward():
            oz = z + r

            @pl.when(z > 0)
            def _():
                self.line_copy(oz, 0).wait_recv()
                total = self.kept[3, oz].astype(F32) + self.up[oz].astype(F32)
                self.kept[3, oz] = total.astype(BF16)

            self.line_copy(oz, 0).start()

        def downward():
            oz = z - r

            @pl.when(z < LINE - 1)
            def _():
                self.line_copy(oz, 1).wait_recv()
                total = self.kept[3, oz].astype(F32) + self.down[oz].astype(F32)
                self.kept[3, oz] = total.astype(BF16)

            self.line_copy(oz, 1).start()

        pl.when(z + r < LINE)(upward)
        pl.when(z - r >= 0)(downward)

    def finish(self):
        z = self.place[0]
        self.out[...] = self.kept[3, z].astype(F32)

        @pl.when(z > 0)
        def _():
            self.line_copy(z, 0).wait_recv()
            self.out[...] += self.up[z].astype(F32)

        @pl.when(z < LINE - 1)
        def _():
            self.line_copy(z, 1).wait_recv()
            self.out[...] += self.down[z].astype(F32)

        for k in range(4):
            self.to_twin(k).wait_send()
        for half in range(2):
            self.corner_copy(half).wait_send()
        for k in (1, 2):
            self.side_copy(k).wait_send()
        for r in range(1, LINE):
            pl.when(z + r < LINE)(lambda r=r: self.line_copy(z + r, 0).wait_send())
            pl.when(z - r >= 0)(lambda r=r: self.line_copy(z - r, 1).wait_send())

    def steps(self):
        return [
            self.begin, self.corners, self.sides_out, self.sides_in, lambda: self.line(3), lambda: self.line(2),
            lambda: self.line(1), self.finish,
        ]


def scatter_scratch(rows, columns):
    dma = pltpu.SemaphoreType.DMA
    half = rows // 2
    return [
        pltpu.VMEM((4, LINE, rows, columns), BF16),
        pltpu.VMEM((4, LINE, rows, columns), BF16),
        pltpu.VMEM((LINE, half, columns), BF16),
        pltpu.VMEM((LINE, half, columns), BF16),
        pltpu.VMEM((LINE, rows, columns), BF16),
        pltpu.VMEM((LINE, rows, columns), BF16),
        pltpu.VMEM((LINE, rows, columns), BF16),
        pltpu.VMEM((LINE, rows, columns), BF16),
        dma((4,)), dma((4,)), dma((4,)), dma((4,)), dma((2, LINE)), dma((2, LINE)),
    ]


class Total:
    def __init__(self, own, out, held, got, sent, recv):
        self.own, self.out, self.held, self.got, self.sent, self.recv = own, out, held, got, sent, recv

    def copy(self, k):
        z, y, x, core = my_place()
        near = z + 1 - 2 * (z % 2)
        peer = [
            (z, y, x, 1 - core), (z, y, 1 - x, core), (z, 1 - y, x, core), (near, y, x, core),
            ((z + 2) % LINE, y, x, core),
        ][k]
        return send(self.own if k == 0 else self.held.at[k], self.got.at[k], self.sent.at[k], self.recv.at[k], peer)

    def begin(self):
        self.copy(0).start()

    def turn(self, k):
        self.copy(k).wait_recv()
        mine = self.own[...] if k == 0 else self.held[k]
        total = mine + self.got[k]
        if k < 4:
            self.held[k + 1] = total
            self.copy(k + 1).start()
        else:
            self.out[...] = total

    def finish(self):
        for k in range(5):
            self.copy(k).wait_send()

    def steps(self):
        return [self.begin] + [lambda k=k: self.turn(k) for k in range(5)] + [self.finish]


def scatter_kernel(count, *refs):
    parts, small = refs[:count], refs[count]
    outs, small_out = refs[count + 1 : 2 * count + 1], refs[2 * count + 1]
    scratch = refs[2 * count + 2 :]
    z, y, x, core = my_place()
    meet([((z + 2) % LINE, y, x, core)])
    lists = []
    for k in range(count):
        own = scratch[14 * k : 14 * k + 14]
        lists.append(Scatter(parts[k], outs[k], None, *own[:8], own[8:]).steps())
    lists.append(Total(small, small_out, *scratch[14 * count :]).steps())
    for at in range(max(len(each) for each in lists)):
        for each in lists:
            if at < len(each):
                each[at]()


def scattered(arrays, small, number):
    count = len(arrays)
    shapes = [(a.shape[0] // 32, a.shape[1]) for a in arrays]
    dma = pltpu.SemaphoreType.DMA
    scratch = []
    for shape in shapes:
        scratch += scatter_scratch(*shape)
    scratch += [
        pltpu.VMEM((5,) + small.shape, F32), pltpu.VMEM((5,) + small.shape, F32), dma((5,)), dma((5,)),
    ]
    vmem = pl.BlockSpec(memory_space=pltpu.VMEM)
    return pl.pallas_call(
        lambda *refs: scatter_kernel(count, *refs),
        in_specs=[vmem] * (count + 1),
        out_specs=[vmem] * (count + 1),
        out_shape=[shaped(shape, F32) for shape in shapes] + [shaped(small.shape, F32)],
        scratch_shapes=scratch,
        compiler_params=pltpu.CompilerParams(
            collective_id=number, has_side_effects=True, vmem_limit_bytes=60 * 1024 * 1024
        ),
        name="scatter",
    )(*[a.reshape(LINE, 2, 2, 2, s[0], s[1]) for a, s in zip(arrays, shapes)], small)


def local(
    tokens,
    valid_mask,
    stretch_start,
    cotangent,
    norm_gain,
    in_weight,
    conv_weight,
    conv_bias,
    step_bias,
    decay_log,
    skip_gain,
    gate_gain,
    out_weight,
):
    axes = ("fsdp", "ctx")
    rows, width = tokens.shape
    blocks = rows // Q
    near = lax.axis_size("ctx")
    pos = lax.axis_index("ctx").astype(jnp.int32).reshape(1, 1)
    halo_tokens = lax.ppermute(
        tokens[rows - 8 :], "ctx", [(k, k + 1) for k in range(near - 1)]
    )
    own_u = jnp.pad(in_weight[:, DI:], ((0, 0), (0, UW - (DPROJ - DI))))
    own_z = in_weight[:, :DI]
    boxed = lax.axis_size("fsdp") == 8 and near == 4
    if boxed:
        w_u, w_z, w_o = gathered([own_u, own_z, out_weight], 1)
    else:
        w_u, w_z, w_o = [lax.all_gather(a, axes, axis=0, tiled=True) for a in (own_u, own_z, out_weight)]

    def hats(values):
        wide = values.astype(F32)
        return wide * lax.rsqrt(jnp.mean(wide * wide, axis=-1, keepdims=True) + epsilon)

    normed_more = (hats(jnp.concatenate([tokens, halo_tokens], 0)) * norm_gain).astype(BF16)
    normed = normed_more[:rows]
    valid = jnp.broadcast_to(valid_mask.astype(F32)[:, None], (rows, 128))
    keep = (1.0 - stretch_start[0].astype(F32)).reshape(1, 1)
    taps = conv_weight
    shift = conv_bias.reshape(1, CH)
    bias = jnp.pad(step_bias, (0, 128 - HEADS)).reshape(1, 128)
    logs = jnp.pad(decay_log, (0, 128 - HEADS)).reshape(1, 128)
    skips = jnp.repeat(skip_gain, P_SIZE).reshape(1, DI)
    u = jnp.dot(normed_more, w_u, preferred_element_type=F32)
    halo_block = rows // 8

    same = lambda c: (c, 0)
    same3 = lambda c: (c, 0, 0)
    val, vp, conv, bc, ssd, ent, logd, step, cum, fin = pl.pallas_call(
        forward_kernel,
        grid=(blocks,),
        in_specs=[
            spec((Q, UW), same),
            spec((8, UW), lambda c: (halo_block, 0)),
            spec((Q, 128), same),
            scalar(),
            whole((CONVK, CH)),
            whole((1, CH)),
            whole((1, 128)),
            whole((1, 128)),
            whole((1, DI)),
        ],
        out_specs=[
            spec((Q, DI), same),
            spec((Q, DI), same),
            spec((Q, CH), same),
            spec((Q, 2 * N), same),
            spec((Q, DI), same),
            spec((1, N, DI), same3),
            spec((Q, 128), same),
            spec((Q, 128), same),
            whole((blocks + 1, 8, DI)),
            whole((N + 16, DI)),
        ],
        out_shape=[
            shaped((rows, DI), BF16),
            shaped((rows, DI), BF16),
            shaped((rows, CH), BF16),
            shaped((rows, 2 * N), BF16),
            shaped((rows, DI), BF16),
            shaped((blocks, N, DI), BF16),
            shaped((rows, 128), F32),
            shaped((rows, 128), F32),
            shaped((blocks + 1, 8, DI), F32),
            shaped((N + 16, DI), BF16),
        ],
        scratch_shapes=[
            pltpu.VMEM((Q + 8, CH), F32),
            pltpu.VMEM((GROUPS, Q, 128), F32),
            pltpu.VMEM((GROUPS, Q, 128), F32),
            pltpu.VMEM((GROUPS, 8, Q), F32),
            pltpu.VMEM((Q, Q), F32),
            pltpu.VMEM((N, DI), F32),
        ],
        compiler_params=params(),
        cost_estimate=cost(15e9, 60e6),
        name="forward",
    )(u, u, valid, keep, taps, shift, bias, logs, skips)

    z = jnp.dot(normed, w_z, preferred_element_type=F32).astype(BF16)
    everyone = lax.all_gather(fin, "ctx")
    back = lambda i: (blocks - 1 - i, 0)
    back3 = lambda i: (blocks - 1 - i, 0, 0)
    gains = gate_gain.reshape(1, DI)
    output, gated, branch_grad, ds, dz, entt, gnext, gout, dlp, dc, gate_sums = pl.pallas_call(
        gate_kernel,
        grid=(blocks,),
        in_specs=[
            scalar(),
            scalar(),
            whole((near, N, DI)),
            spec((near, 16, DI), lambda i: (0, N // 16, 0)),
            spec((Q, DI), back),
            spec((1, N, DI), back3),
            spec((Q, DI), back),
            spec((Q, DI), back),
            spec((Q, 2 * N), back),
            spec((Q, 128), back),
            whole((blocks + 1, 8, DI)),
            spec((Q, width), back),
            spec((Q, width), back),
            spec((Q, 128), back),
            whole((DI, width)),
            whole((1, DI)),
        ],
        out_specs=[
            spec((Q, width), back),
            spec((Q, DI), back),
            spec((Q, width), back),
            spec((Q, DI), back),
            spec((Q, DI), back),
            spec((1, N, DI), back3),
            spec((1, N, DI), back3),
            whole((N, DI)),
            spec((Q, 128), back),
            spec((Q, N), back),
            whole((8, DI)),
        ],
        out_shape=[
            shaped((rows, width), BF16),
            shaped((rows, DI), BF16),
            shaped((rows, width), BF16),
            shaped((rows, DI), BF16),
            shaped((rows, DI), BF16),
            shaped((blocks, N, DI), BF16),
            shaped((blocks, N, DI), BF16),
            shaped((N, DI), BF16),
            shaped((rows, 128), F32),
            shaped((rows, N), F32),
            shaped((8, DI), F32),
        ],
        scratch_shapes=[
            pltpu.VMEM((N, DI), F32),
            pltpu.VMEM((N, DI), F32),
            pltpu.VMEM((GROUPS, Q, 128), F32),
            pltpu.VMEM((Q, DI), F32),
            pltpu.VMEM((Q, DI), F32),
            pltpu.VMEM((Q, DI), F32),
            pltpu.VMEM((Q, DI), F32),
            pltpu.VMEM((Q, DI), F32),
            pltpu.VMEM((Q, 128), F32),
        ],
        compiler_params=params(),
        cost_estimate=cost(15e9, 60e6),
        name="gate",
    )(
        pos, keep, everyone, everyone, ssd, ent, z, val, bc, logd, cum, tokens, cotangent, valid, w_o, gains,
    )
    everyone_back = lax.all_gather(gout, "ctx")

    dvp, dbc, dlt = pl.pallas_call(
        mixing_kernel,
        grid=(blocks,),
        in_specs=[
            spec((Q, DI), same),
            spec((Q, DI), same),
            spec((Q, 2 * N), same),
            spec((Q, 128), same),
        ],
        out_specs=[spec((Q, DI), same), spec((Q, 2 * N), same), spec((Q, 128), same)],
        out_shape=[shaped((rows, DI), BF16), shaped((rows, 2 * N), F32), shaped((rows, 128), F32)],
        scratch_shapes=[
            pltpu.VMEM((GROUPS, Q, 128), F32),
            pltpu.VMEM((GROUPS, 8, Q), F32),
            pltpu.VMEM((Q, Q), F32),
            pltpu.VMEM((Q, Q), F32),
            pltpu.VMEM((GROUPS, 8, Q), F32),
            pltpu.VMEM((128, Q), F32),
            pltpu.VMEM((GROUPS, Q, 128), F32),
        ],
        compiler_params=params(),
        cost_estimate=cost(15e9, 60e6),
        name="mixing",
    )(ds, vp, bc, logd)

    def columns_of(left, right):
        return lax.dot_general(
            left, right, (((0,), (0,)), ((), ())), preferred_element_type=F32
        ).astype(BF16)

    out_weight_grad = columns_of(gated, branch_grad)
    gate_columns = columns_of(normed, dz)

    du, last, edge, conv_sums, small = pl.pallas_call(
        back_kernel,
        grid=(blocks,),
        in_specs=[
            scalar(),
            scalar(),
            whole((near, N, DI)),
            spec((near, 16, DI), lambda i: (0, N // 16, 0)),
            spec((1, N, DI), back3),
            spec((1, N, DI), back3),
            whole((blocks + 1, 8, DI)),
            spec((Q, DI), back),
            spec((Q, DI), back),
            spec((Q, DI), back),
            spec((Q, DI), back),
            spec((Q, CH), back),
            spec((Q, UW), back),
            spec((8, UW), lambda i: (halo_block, 0)),
            spec((Q, 2 * N), back),
            spec((Q, 128), back),
            spec((Q, 128), back),
            spec((Q, 128), back),
            spec((Q, 128), back),
            spec((Q, 128), back),
            spec((Q, 2 * N), back),
            spec((Q, N), back),
            whole((CONVK, CH)),
            whole((1, 128)),
            whole((1, 128)),
            whole((1, DI)),
        ],
        out_specs=[
            spec((Q, UW), back),
            whole((8, CH)),
            whole((8, CH)),
            whole((8, CH)),
            whole((8, 128)),
        ],
        out_shape=[
            shaped((rows, UW), BF16),
            shaped((8, CH), F32),
            shaped((8, CH), F32),
            shaped((8, CH), F32),
            shaped((8, 128), F32),
        ],
        scratch_shapes=[
            pltpu.VMEM((N, DI), F32),
            pltpu.VMEM((GROUPS, Q, 128), F32),
            pltpu.VMEM((GROUPS, Q, 128), F32),
            pltpu.VMEM((Q + 8, CH), F32),
            pltpu.VMEM((8, CH), F32),
            pltpu.VMEM((16, CH), F32),
            pltpu.VMEM((Q, 128), F32),
            pltpu.VMEM((Q, 128), F32),
            pltpu.VMEM((16, 128), F32),
        ],
        compiler_params=params(),
        cost_estimate=cost(15e9, 60e6),
        name="back",
    )(
        pos, keep, everyone_back, everyone, gnext, entt, cum, vp, val, dvp, ds, conv, u, u, bc, logd, step, valid,
        dlp, dlt, dbc, dc, taps, bias, logs, skips,
    )
    edge_back = lax.ppermute(edge, "ctx", [(k + 1, k) for k in range(near - 1)])
    du = lax.dynamic_update_slice(du, (last + edge_back).astype(BF16), (rows - 8, 0))
    conv_columns = columns_of(normed, du)
    across = (((1,), (1,)), ((), ()))
    normed_grad = lax.dot_general(dz, w_z, across, preferred_element_type=F32) + lax.dot_general(
        du, w_u, across, preferred_element_type=F32
    )
    inputs = tokens.astype(F32)
    scale = lax.rsqrt(jnp.mean(inputs * inputs, axis=-1, keepdims=True) + epsilon)
    hat = inputs * scale
    inner = normed_grad * norm_gain
    input_grad = cotangent.astype(F32) + scale * (
        inner - hat * jnp.mean(inner * hat, axis=-1, keepdims=True)
    )
    norm_grad = jnp.sum(normed_grad * hat, axis=0)
    packed = jnp.concatenate(
        [
            norm_grad,
            conv_sums[:5].reshape(-1),
            gate_sums[:2].reshape(-1),
            small[:2].reshape(-1),
        ]
    )
    if boxed:
        conv_columns, gate_columns, out_weight_grad, summed = scattered(
            [conv_columns, gate_columns, out_weight_grad], packed.reshape(-1, 128), 2
        )
        summed = summed.reshape(-1)
    else:
        conv_columns, gate_columns, out_weight_grad = [
            lax.psum_scatter(a.astype(F32), axes, scatter_dimension=0, tiled=True)
            for a in (conv_columns, gate_columns, out_weight_grad)
        ]
        summed = lax.psum(packed, axes)
    in_weight_grad = jnp.concatenate([gate_columns, conv_columns[:, : DPROJ - DI]], 1)
    at = width
    conv_weight_grad = summed[at : at + CONVK * CH].reshape(CONVK, CH)
    at += CONVK * CH
    conv_bias_grad = summed[at : at + CH]
    at += CH
    gate_gain_grad = summed[at : at + DI]
    at += DI
    skip_gain_grad = jnp.sum(summed[at : at + DI].reshape(HEADS, P_SIZE), axis=1)
    at += DI
    step_bias_grad = summed[at : at + HEADS]
    decay_log_grad = summed[at + 128 : at + 128 + HEADS]
    return (
        output,
        input_grad,
        in_weight_grad,
        out_weight_grad,
        summed[:width],
        conv_weight_grad,
        conv_bias_grad,
        step_bias_grad,
        decay_log_grad,
        skip_gain_grad,
        gate_gain_grad,
    )


def solution(mesh):
    split = P(("fsdp", "ctx"), None)
    line = P(("fsdp", "ctx"))
    return jax.shard_map(
        local,
        mesh=mesh,
        in_specs=(split, line, line, split, P(), split, P(), P(), P(), P(), P(), P(), split),
        out_specs=(split, split, split, split, P(), P(), P(), P(), P(), P(), P()),
        check_vma=False,
    )
```

time: 879 us -> 487 us (0.55)
  Pallas kernels: 0 us -> 359 us
  other arithmetic: 222 us -> 14.3 us
  waiting for transfers between devices: 204 us -> 14 us
  local copies, waits for them, and re-layouts: 192 us -> 18.8 us
  matrix products: 174 us -> 58 us
  blocking collectives: 57.1 us -> 0 us
    pallas_call x0 -> x6, Pallas kernels: none -> 359 us  [the longest x1 99.8 us: scattered(): pl.pallas_call(lambda *refs: scatter_kernel(count, *refs), in_specs=[vmem...]
    reduce_scatter x2 -> x0, waiting for transfers between devices: 123 us -> none  [the longest x1 123 us: local(): lax.psum_scatter(lax.dot_general(columns, projected_low, (((0,), (0,)), (...]
    dot_general x20 -> x7, matrix products: 174 us -> 58 us  [the longest x3 24.8 us: columns_of(): lax.dot_general(left, right, (((0,), (0,)), ((), ())), preferred_element_...]
    all_gather x4 -> x2, waiting for transfers between devices: 79.8 us -> 13.4 us  [the longest x1 13.4 us: local(): everyone = lax.all_gather(fin, 'ctx')]
    reshape x4 -> x6, local copies, waits for them, and re-layouts: 62.6 us -> 4.79 us  [the longest x1 1.31 us: local(): shift = conv_bias.reshape(1, CH)]
    reduce_sum x9 -> x3, other arithmetic: 54.5 us -> 3.34 us  [the longest x1 2.24 us: hats(): jnp.mean(wide * wide, axis=-1, keepdims=True) + epsilon]
    add_any x4 -> x0, other arithmetic: 45.2 us -> none  [the longest x1 20.8 us: first_section(): padded[:, offset:offset + width]]
    psum x1 -> x0, blocking collectives: 43.5 us -> none  [local(): lax.psum((norm_grad, firsts_grad[2], firsts_grad[3], firsts_grad[4], firs...]
  transfers between devices with their start and end apart: 8 -> 4, of which waited for: 2 -> 2; matrix products, arithmetic and copies ran while one was open for 49% -> 8% of each run, Pallas kernels for 0% -> 20%
where the time goes in v1:
time: 487 us; the launch traced here: 483 us
  Pallas kernels  359 us (74%)
  matrix products  58 us (12%)
  local copies, waits for them, and re-layouts  18.8 us (4%)
  between operations  15.1 us (3%)
  other arithmetic  14.3 us (3%)
  waiting for transfers between devices  14 us (3%)
    pallas_call x1, Pallas kernels, scattered(): pl.pallas_call(lambda *refs: scatter_kernel(count, *refs), in_specs=[vmem...  99.8 us
    pallas_call x1, Pallas kernels, gathered(): pl.pallas_call(lambda *refs: gather_kernel(count, *refs), in_specs=[anywh...  70.6 us
    pallas_call x1, Pallas kernels, local(): pl.pallas_call(back_kernel, grid=(blocks,), in_specs=[scalar(), scalar(),...  62 us
    pallas_call x1, Pallas kernels, local(): pl.pallas_call(gate_kernel, grid=(blocks,), in_specs=[scalar(), scalar(),...  55.5 us
    pallas_call x1, Pallas kernels, local(): pl.pallas_call(forward_kernel, grid=(blocks,), in_specs=[spec((Q, UW), sa...  44.6 us
    pallas_call x1, Pallas kernels, local(): pl.pallas_call(mixing_kernel, grid=(blocks,), in_specs=[spec((Q, DI), sam...  26.4 us
    dot_general x3, matrix products, columns_of(): lax.dot_general(left, right, (((0,), (0,)), ((), ())), preferred_element_...  24.8 us
    all_gather x1, waiting for transfers between devices, local(): everyone = lax.all_gather(fin, 'ctx')  13.4 us
  transfers between devices with their start and end apart: 4, of which 2 were waited for; matrix products, arithmetic and copies ran while one was open for 8% of the time, Pallas kernels for 20%

profile of v1, /device:TPU:0, one launch (start us, length us, event | category | flops | bytes accessed | tf_op | source)
XLA Modules:
  0.0 482.8 jit_solution(5375131786581452428)
XLA Ops:
  7.2 0.9 slice.60
  8.1 2.4 collective-permute-start
  10.5 1.2 pad_bitcast_fusion
  11.7 0.9 slice.61
  12.6 1.6 slice.62.refs_1_
  16.9 1.3 reshape.105.cb_ref
  18.9 70.6 %gather.1 = (bf16[1024,2432]{1,0:T(8,128)(2,1)}, bf16[1024,2048]{1,0:T(8,128)(2,1)}, bf16[2048,1024]{1,0:T(8,128)(2,1)}) custom-call(bf16[32,2432]{1,0:T(8,128)(2,1)} %pad.11.refs_0_, bf16[32,2048]{1,0:T(8,128)(2,1)} %slice.62.refs_1_, bf16[64,1024]{1,0:T(8,128)(2,1)} %refs_2_.1), custom_call_target="tpu_custom_call" | custom-call | tf_op jit(solution)/shard_map/gather/pallas_call | solution.py:760
  89.6 2.2 fusion.3
  91.8 1.2 fusion.5
  93.1 8.2 %fusion.17.u_ref.halo_ref = f32[1032,2432]{1,0:T(8,128)} fusion(bf16[1032,1024]{1,0:T(8,128)(2,1)S(1)} %fusion.5, bf16[1024,2432]{1,0:T(8,128)(2,1)S(1)} %copy-done.6), kind=kOutput, calls=%fused_computation.40 | convolution fusion | flops 5140119552 | bytes 17133568 | tf_op jit(solution)/shard_map/dot_general | solution.py:1045
  101.2 1.0 broadcast_in_dim.4.valid_ref
  102.2 44.6 %forward.1 = (bf16[1024,2048]{1,0:T(8,128)(2,1)}, bf16[1024,2048]{1,0:T(8,128)(2,1)}, bf16[1024,2304]{1,0:T(8,128)(2,1)}, bf16[1024,256]{1,0:T(8,128)(2,1)}, bf1...) custom-call(f32[1032,2432]{1,0:T(8,128)} %fusion.17.u_ref.halo_ref, ...), custom_call_target="tpu_custom_call" | custom-call | flops 15000000512 | bytes 60000000 | tf_op jit(solution)/shard_map/forward/pallas_call | solution.py:1050
  147.5 9.3 %convolution_convert_fusion.3.z_ref = bf16[1024,2048]{1,0:T(8,128)(2,1)} fusion(bf16[1024,2048]{1,0:T(8,128)(2,1)} %get-tuple-element.51, bf16[1032,1024]{1,0:T(8,128)(2,1)} %copy-done.2), kind=kOutput, calls=%fused_computation.19 | convolution fusion | flops 4297064448 | bytes 10485760 | tf_op jit(solution)/shard_map/dot_general | solution.py:1101
  156.8 13.4 %all-gather.5.cloned.1.call-done = bf16[576,2048]{1,0:T(8,128)(2,1)} async-done(((bf16[144,2048]{1,0:T(8,128)(2,1)}), bf16[576,2048]{1,0:T(8,128)(2,1)}) %all-gather.5.cloned.1.call-update) | async-done | bytes 2359312 | tf_op jit(solution)/shard_map/all_gather | solution.py:1102
  170.2 55.5 %gate.1 = (bf16[1024,1024]{1,0:T(8,128)(2,1)}, bf16[1024,2048]{1,0:T(8,128)(2,1)}, bf16[1024,1024]{1,0:T(8,128)(2,1)}, bf16[1024,2048]{1,0:T(8,128)(2,1)}, bf16[...) custom-call(s32[1,1]{1,0:T(1,128)} %bitcast.pos_ref, ...), custom_call_target="tpu_custom_call" | custom-call | flops 15000000512 | bytes 60000000 | tf_op jit(solution)/shard_map/gate/pallas_call | solution.py:1106
  226.6 8.5 %convolution_convert_fusion.2 = bf16[1024,2048]{1,0:T(8,128)(2,1)} fusion(bf16[1024,2048]{1,0:T(8,128)(2,1)} %get-tuple-element.58, bf16[1032,1024]{1,0:T(8,128)(2,1)S(1)} %copy-done.3), kind=kOutput, calls=%fused_computation.18 | convolution fusion | flops 4297064448 | bytes 10485760 | tf_op jit(solution)/shard_map/dot_general | solution.py:1198
  235.2 6.1 %convolution_convert_fusion.1 = bf16[2048,1024]{1,0:T(8,128)(2,1)} fusion(bf16[1024,2048]{1,0:T(8,128)(2,1)S(1)} %copy-done.11, bf16[1024,1024]{1,0:T(8,128)(2,1)S(1)} %copy-done.12), kind=kOutput, calls=%fused_computation.17 | convolution fusion | flops 4297064448 | bytes 10485760 | tf_op jit(solution)/shard_map/dot_general | solution.py:1198
  241.3 6.1 %fusion.18 = f32[1024,1024]{1,0:T(8,128)} fusion(bf16[1024,2048]{1,0:T(8,128)(2,1)S(1)} %copy-done.10, bf16[1024,2048]{1,0:T(8,128)(2,1)S(1)} %copy-done.8), kind=kOutput, calls=%fused_computation.41 | convolution fusion | flops 4294967296 | bytes 12582912 | tf_op jit(solution)/shard_map/dot_general | solution.py:1272
  247.4 26.4 %mixing.1 = (bf16[1024,2048]{1,0:T(8,128)(2,1)}, f32[1024,256]{1,0:T(8,128)}, f32[1024,128]{1,0:T(8,128)}) custom-call(bf16[1024,2048]{1,0:T(8,128)(2,1)} %get-tuple-element.63.ds_ref, bf16[1024,2048]{1,0:T(8,128)(2,1)} %get-tuple-element.62.vp_ref, bf16[1024,256]{1,0:T(8,128)(2,1)} %get-tuple-element.53.bc_ref, f32[1024,128]{1,0:T(8,128)} %get-tuple-element.54.log_ref), custom_call_target="tpu_custom_call" | custom-call | flops 15000000512 | bytes 60000000 | tf_op jit(solution)/shard_map/mixing/pallas_call | solution.py:1172
  273.8 62.0 %back.1 = (bf16[1024,2432]{1,0:T(8,128)(2,1)}, f32[8,2304]{1,0:T(8,128)}, f32[8,2304]{1,0:T(8,128)}, f32[8,2304]{1,0:T(8,128)}, f32[8,128]{1,0:T(8,128)}) custom-call(s32[1,1]{1,0:T(1,128)} %bitcast.pos_ref, f32[1,1]{1,0:T(1,128)} %bitcast.1.keep_ref, bf16[4,128,2048]{2,1,0:T(8,128)(2,1)} %bitcast.50, bf16[4,144,2048]{2,1,0:T(8,128)(2,1)} %bitcast.49, ...), custom_call_target="tpu_custom_call" | custom-call | flops 15000000512 | bytes 60000000 | tf_op jit(solution)/shard_map/back/pallas_call | solution.py:1205
  335.8 1.3 collective-permute-start.1
  337.7 0.9 reshape.112
  339.1 1.5 fusion.15
  340.7 10.2 %convolution_convert_fusion = bf16[1024,2432]{1,0:T(8,128)(2,1)} fusion(bf16[1024,2432]{1,0:T(8,128)(2,1)} %fusion.15, bf16[1032,1024]{1,0:T(8,128)(2,1)} %copy-done.2), kind=kOutput, calls=%fused_computation | convolution fusion | flops 5102764032 | bytes 12058624 | tf_op jit(solution)/shard_map/dot_general | solution.py:1198
  350.9 9.6 %fusion.10 = (f32[1024]{0:T(1024)S(1)}, f32[1024]{0:T(1024)S(1)}, f32[1024,1024]{1,0:T(8,128)}) fusion(bf16[1024,1024]{1,0:T(8,128)(2,1)S(1)} %copy-done.1, f32[1024]{0:T(1024)S(1)} %add_rsqrt_fusion.1, f32[1024]{0:T(1024)S(1)} %copy-done.5, f32[1024,1024]{1,0:T(8,128)S(1)} %copy-done.9, bf16[1024,2432]{1,0:T(8,128)(2,1)S(1)} %copy-done.7, ...), kind=kOutput, calls=%fused_computation.15 | convolution fusion | flops 5108660224 | bytes 20463616 | tf_op jit(solution)/shard_map/dot_general | solution.py:1272
  361.1 99.8 %scatter.1 = (f32[32,2432]{1,0:T(8,128)}, f32[32,2048]{1,0:T(8,128)}, f32[64,1024]{1,0:T(8,128)}, f32[132,128]{1,0:T(8,128)}) custom-call(bf16[4,2,2,2,32,2432]{5,4,3,2,1,0:T(8,128)(2,1)} %bitcast.40, bf16[4,2,2,2,32,2048]{5,4,3,2,1,0:T(8,128)(2,1)} %bitcast.41, bf16[4,2,2,2,64,1024]{5,4,3,2,1,0:T(8,128)(2,1)} %bitcast.42, ...), custom_call_target="tpu_custom_call" | custom-call | tf_op jit(solution)/shard_map/scatter/pallas_call | solution.py:988
  461.7 1.4 slice_bitcast_fusion.2
  463.1 1.3 slice_bitcast_fusion.1
  464.4 1.3 slice_bitcast_fusion.3
  466.4 1.3 fusion.16
  467.6 1.9 pad_maximum_fusion.1
  470.1 5.0 %fusion.9 = f32[1024,1024]{1,0:T(8,128)} fusion(bf16[1024,1024]{1,0:T(8,128)(2,1)S(1)} %copy-done.1, bf16[1024,1024]{1,0:T(8,128)(2,1)} %cot_ref.1, f32[1024,1024]{1,0:T(8,128)} %get-tuple-element.89, f32[1024]{0:T(1024)S(1)} %broadcast_multiply_fusion, f32[1024]{0:T(1024)S(1)} %copy-done.5, f32[1024]{0:T(1024)S(1)} %add_rsqrt_fusion.1), kind=kLoop, calls=%fused_computation.14 | loop fusion | flops 8388608 | bytes 12595200 | tf_op jit(solution)/shard_map/add | solution.py:1279
  (50 shorter events, 8.9 us)
Async XLA Ops:
  7.2 84.6 %copy-start = (bf16[1024,1024]{1,0:T(8,128)(2,1)S(1)}, bf16[1024,1024]{1,0:T(8,128)(2,1)}, u32[]{:S(2)}) copy-start(bf16[1024,1024]{1,0:T(8,128)(2,1)} %tok_ref.1) | copy-start | bytes 6291460
  7.2 163.0 %all-gather.5.cloned.1.call-start = ((), (), s32[]{:S(2)}) async-start(), calls=%async_computation | async-start | bytes 2949120 | tf_op jit(solution)/shard_map/all_gather | solution.py:1102
  8.1 81.5 %collective-permute-start = (bf16[8,1024]{1,0:T(8,128)(2,1)S(1)}, bf16[8,1024]{1,0:T(8,128)(2,1)S(1)}, u32[]{:S(2)}, u32[]{:S(2)}) collective-permute-start(bf16[8,1024]{1,0:T(8,128)(2,1)S(1)} %slice.60), channel_id=1, source_target_pairs={{0,1},{1,2},{2,3},{4,5},{5,6},{6,7},{8,9},{9,10},{10,11},{12,13},{... | collective-permute-start | bytes 49160 | tf_op jit(solution)/shard_map/ppermute | solution.py:1021
  89.5 3.5 copy-start.6
  93.1 8.2 %copy-start.2 = (bf16[1032,1024]{1,0:T(8,128)(2,1)}, bf16[1032,1024]{1,0:T(8,128)(2,1)S(1)}, u32[]{:S(2)}) copy-start(bf16[1032,1024]{1,0:T(8,128)(2,1)S(1)} %fusion.5) | copy-start | bytes 6340612
  146.9 126.9 %all-gather.7.cloned.1.call-start = ((), (), s32[]{:S(2)}) async-start(), calls=%async_computation.1 | async-start | bytes 2621440 | tf_op jit(solution)/shard_map/all_gather | solution.py:1170
  170.2 56.4 %copy-start.3 = (bf16[1032,1024]{1,0:T(8,128)(2,1)S(1)}, bf16[1032,1024]{1,0:T(8,128)(2,1)}, u32[]{:S(2)}) copy-start(bf16[1032,1024]{1,0:T(8,128)(2,1)} %copy-done.2) | copy-start | bytes 6340612
  226.6 8.5 %copy-start.11 = (bf16[1024,2048]{1,0:T(8,128)(2,1)S(1)}, bf16[1024,2048]{1,0:T(8,128)(2,1)}, u32[]{:S(2)}) copy-start(bf16[1024,2048]{1,0:T(8,128)(2,1)} %get-tuple-element.74) | copy-start | bytes 12582916
  226.6 8.5 %copy-start.12 = (bf16[1024,1024]{1,0:T(8,128)(2,1)S(1)}, bf16[1024,1024]{1,0:T(8,128)(2,1)}, u32[]{:S(2)}) copy-start(bf16[1024,1024]{1,0:T(8,128)(2,1)} %get-tuple-element.75) | copy-start | bytes 6291460
  235.1 6.1 %copy-start.8 = (bf16[1024,2048]{1,0:T(8,128)(2,1)S(1)}, bf16[1024,2048]{1,0:T(8,128)(2,1)}, u32[]{:S(2)}) copy-start(bf16[1024,2048]{1,0:T(8,128)(2,1)} %get-tuple-element.51) | copy-start | bytes 12582916
  235.2 6.1 %copy-start.10 = (bf16[1024,2048]{1,0:T(8,128)(2,1)S(1)}, bf16[1024,2048]{1,0:T(8,128)(2,1)}, u32[]{:S(2)}) copy-start(bf16[1024,2048]{1,0:T(8,128)(2,1)} %get-tuple-element.58) | copy-start | bytes 12582916
  335.8 3.4 collective-permute-start.1
  340.6 10.2 %copy-start.1 = (bf16[1024,1024]{1,0:T(8,128)(2,1)S(1)}, bf16[1024,1024]{1,0:T(8,128)(2,1)}, u32[]{:S(2)}) copy-start(bf16[1024,1024]{1,0:T(8,128)(2,1)} %tok_ref.1) | copy-start | bytes 6291460
  340.6 10.2 %copy-start.5 = (f32[1024]{0:T(1024)S(1)}, f32[1024]{0:T(1024)}, u32[]{:S(2)}) copy-start(f32[1024]{0:T(1024)} %param.17) | copy-start | bytes 12292
  340.6 10.2 %copy-start.7 = (bf16[1024,2432]{1,0:T(8,128)(2,1)S(1)}, bf16[1024,2432]{1,0:T(8,128)(2,1)}, u32[]{:S(2)}) copy-start(bf16[1024,2432]{1,0:T(8,128)(2,1)} %fusion.15) | copy-start | bytes 14942212
  340.6 10.2 %copy-start.9 = (f32[1024,1024]{1,0:T(8,128)S(1)}, f32[1024,1024]{1,0:T(8,128)}, u32[]{:S(2)}) copy-start(f32[1024,1024]{1,0:T(8,128)} %fusion.18) | copy-start | bytes 12582916
  470.1 5.0 %copy-start.4 = (f32[64,1024]{1,0:T(8,128)S(1)}, f32[64,1024]{1,0:T(8,128)}, u32[]{:S(2)}) copy-start(f32[64,1024]{1,0:T(8,128)} %get-tuple-element.106) | copy-start | bytes 786436
Sparse Core Ops, SparseCore 0:
  147.0 23.1 all-gather.4
  225.9 22.5 all-gather.6
